TPU v7x, 32 devices: a whole 2x2x4 slice. The times are simulated.
32 devices in a mesh: row: 4 (over x, core), col: 4 (over z), inner: 2 (over y).
Axes of the slice: x: 2, y: 2, z: 4, core: 2. Of those that a mesh axis runs over, the one named last changes fastest.
Arguments:
- near_flags: int32 [4, 6], P('row', 'inner'), may hold values 0 or 1
- row_factor: bfloat16 [4, 6, 64, 2048], P('row', 'inner', None, 'col'), may hold values from -6 to 6
- col_factor: bfloat16 [4, 6, 64, 2048], P('row', 'inner', None, 'col'), may hold values from -0.0068359375 to 0.0068359375
- near_block: bfloat16 [4, 6, 2048, 2048], P('row', 'inner', None, 'col'), may hold values from -0.0546875 to 0.0546875
- inner_left: bfloat16 [6, 16, 64, 2048], P('inner', 'col', None, 'row'), may hold values from -6 to 6
- inner_right: bfloat16 [6, 16, 64, 2048], P('inner', 'col', None, 'row'), may hold values from -0.75 to 0.75
- sketch_matrix: bfloat16 [16, 64, 2048], P('col'), may hold values from -0.125 to 0.125
Outputs:
- basis: float32 [4, 16, 64, 2048], P('row', 'col', None, 'inner')
- coupling: float32 [4, 16, 64, 2048], P('row', 'col', None, 'inner')
Inputs may be any that keep to these rules, and one draw needn't show every extreme that they name: `near_flags`: 1 marks a near-field block.
All inputs are finite; a program needn't handle non-finite values.
Results may differ from a plain program's by a relative error of at most 0.0055.
Values may be sent and summed in bfloat16 or wider, within the bound.
A program may use at most 128 MiB of HBM per device.

v0:
```python
import functools
import math

import jax
import jax.numpy as jnp
from jax import lax
from jax.experimental import pallas as pl
from jax.experimental.pallas import tpu as pltpu
from jax.sharding import PartitionSpec as P

MESH = pl.DeviceIdType.MESH
HIGHEST = lax.Precision.HIGHEST
WIDE = jnp.float32
NARROW = jnp.bfloat16


def remote(src, dst, sems, slot, device):
    return pltpu.make_async_remote_copy(
        src_ref=src, dst_ref=dst, send_sem=sems[0].at[slot], recv_sem=sems[1].at[slot],
        device_id=device, device_id_type=MESH,
    )


def meet(devices):
    barrier = pltpu.get_barrier_semaphore()
    for device in devices:
        pl.semaphore_signal(barrier, inc=1, device_id=device, device_id_type=MESH)
    pl.semaphore_wait(barrier, len(devices))


def gather_kernel(dims, left_ref, right_ref, cols_ref, xg, yg, yi, vg, stage, send, recv, own):
    n_row, n_col, n_in, slots, js, width, rank, cols = dims
    share = yi.shape[-1]
    row, col, inner = lax.axis_index("row"), lax.axis_index("col"), lax.axis_index("inner")
    twin_row = row + 1 - 2 * lax.rem(row, 2)
    far_row = lax.rem(row + 2, n_row)
    sems = (send, recv)
    twin = {"row": twin_row}
    far = {"row": far_row}
    up = {"col": lax.rem(col + 1, n_col)}
    down = {"col": lax.rem(col + n_col - 1, n_col)}
    inner_peers = [lax.rem(inner + d, n_in) for d in range(1, n_in)]
    meet([twin, far, up, down] + [{"inner": p} for p in inner_peers])

    started = []

    def push(src, dst, device):
        copy = remote(src, dst, sems, len(started), device)
        copy.start()
        started.append(copy)
        return copy

    def x_place(r):
        def place(k, c, part=None):
            first, length = (0, js) if part is None else (part * (js // 2), js // 2)
            return xg.at[
                k,
                pl.ds(pl.multiple_of(c * js + first, js // 2), length),
                pl.ds(pl.multiple_of(r * width, width), width),
            ]

        return place

    def y_place(r):
        return yg.at[:, :, pl.ds(pl.multiple_of(r * width, width), width)]

    def v_place(k, c, part=None):
        rows = pl.ds(0, rank) if part is None else pl.ds(part * (rank // 2), rank // 2)
        return vg.at[:, rows, pl.ds(pl.multiple_of(c * cols, cols), cols)]

    half = n_col // 2
    twins = []

    def ring_start(src, place, k):
        spot = place(k, col)
        return (push(src, spot, up), push(src, spot, down))

    def ring_step(pair, place, k, step, relay):
        got_up, got_down = pair
        from_up = lax.rem(col + n_col - step, n_col)
        from_down = lax.rem(col + step, n_col)
        nexts = []
        for got, source, device, part in ((got_up, from_up, up, 0), (got_down, from_down, down, 1)):
            got.wait_recv()
            here = place(k, source, None if step < half else part)
            if step < half:
                on = place(k, source, part) if step + 1 == half else here
                nexts.append(push(on, on, device))
            if relay:
                twins.append(push(here, here, twin))
        return tuple(nexts)

    near, other = x_place(row), x_place(far_row)
    y_far = push(right_ref, y_place(row), far)
    near_rings, far_got = [], []
    for k in range(slots):
        near_rings.append(ring_start(left_ref.at[k], near, k))
        far_got.append(push(left_ref.at[k], near(k, col), far))
    v_ring = ring_start(cols_ref, v_place, 0)
    y_twin = push(right_ref, y_place(row), twin)
    for k in range(slots):
        twins.append(push(left_ref.at[k], near(k, col), twin))
    locals_ = [pltpu.make_async_copy(left_ref.at[k], near(k, col), own.at[k]) for k in range(slots)]
    local_y = pltpu.make_async_copy(right_ref, y_place(row), own.at[slots])
    locals_.append(pltpu.make_async_copy(cols_ref, v_place(0, col), own.at[slots + 1]))
    local_y.start()
    for copy in locals_:
        copy.start()
    for k in range(slots):
        near_rings[k] = ring_step(near_rings[k], near, k, 1, True)
    y_far.wait_recv()
    y_twin_far = push(y_place(far_row), y_place(far_row), twin)
    far_rings, y_out = [], []
    for k in range(slots):
        far_got[k].wait_recv()
        spot = other(k, col)
        far_rings.append(ring_start(spot, other, k))
        twins.append(push(spot, spot, twin))
        if k == 0:
            local_y.wait()
            y_twin.wait_recv()
            y_twin_far.wait_recv()
            for peer in inner_peers:
                src = yg.at[:, :, pl.ds(pl.multiple_of(peer * share, share), share)]
                y_out.append(push(src, yi.at[inner], {"inner": peer}))
            fetch = pltpu.make_async_copy(
                yg.at[:, :, pl.ds(pl.multiple_of(inner * share, share), share)], stage, own.at[slots + 2]
            )
            fetch.start()
    v_ring = ring_step(v_ring, v_place, 0, 1, False)
    fetch.wait()
    store = pltpu.make_async_copy(stage, yi.at[inner], own.at[slots + 3])
    store.start()
    for k in range(slots):
        far_rings[k] = ring_step(far_rings[k], other, k, 1, True)
    for step in range(2, half + 1):
        for k in range(slots):
            near_rings[k] = ring_step(near_rings[k], near, k, step, True)
        v_ring = ring_step(v_ring, v_place, 0, step, False)
        for k in range(slots):
            far_rings[k] = ring_step(far_rings[k], other, k, step, True)
    for copy in twins + y_out:
        copy.wait_recv()
    for copy in locals_ + [store]:
        copy.wait()
    for copy in started:
        copy.wait_send()


def gather_all(left, right, cols_own, sizes):
    n_row, n_col, n_in = sizes
    slots, js, width = left.shape
    rank, cols = cols_own.shape[1:]
    total = width * n_row
    half = n_col // 2
    n_copies = 3 + (n_in - 1) + slots * 3 + (2 * slots + 1) * 2 * half + 2 * slots * 2 * half
    dims = (n_row, n_col, n_in, slots, js, width, rank, cols)
    hbm = pl.BlockSpec(memory_space=pltpu.HBM)
    vmem = pl.BlockSpec(memory_space=pltpu.VMEM)
    return pl.pallas_call(
        functools.partial(gather_kernel, dims),
        out_shape=(
            jax.ShapeDtypeStruct((slots, n_col * js, total), left.dtype),
            jax.ShapeDtypeStruct((slots, js, total), left.dtype),
            jax.ShapeDtypeStruct((n_in, slots, js, total // n_in), left.dtype),
            jax.ShapeDtypeStruct((slots, rank, total), left.dtype),
        ),
        in_specs=[vmem] * 3,
        out_specs=[hbm] * 4,
        scratch_shapes=[
            pltpu.VMEM((slots, js, total // n_in), left.dtype),
            pltpu.SemaphoreType.DMA((n_copies,)),
            pltpu.SemaphoreType.DMA((n_copies,)),
            pltpu.SemaphoreType.DMA((slots + 4,)),
        ],
        compiler_params=pltpu.CompilerParams(collective_id=0, has_side_effects=True),
    )(left, right, cols_own)


def spread_kernel(dims, p_ref, z_ref, pr, zr, relay, send, recv, hop_send, hop_recv, on_send, on_recv, zsend, zrecv, own):
    n_col, n_in, group, own_j, cols = dims
    col, inner = lax.axis_index("col"), lax.axis_index("inner")
    half, half_j = n_col // 2, own_j // 2

    def home(c):
        return lax.div(c, group)

    def column(d):
        return lax.rem(col + n_col + d, n_col)

    def window(c, first=0, length=own_j):
        at = pl.multiple_of(lax.rem(c, group) * cols, cols)
        return pr.at[pl.ds(first, length), inner, :, :, pl.ds(at, cols)]

    meet([
        {"col": column(d), "inner": lax.rem(inner + e, n_in)}
        for d in range(n_col) for e in range(n_in) if d or e
    ])
    sides = (1, -1)
    hops = []
    for n, side in enumerate(sides):
        hop = remote(
            p_ref.at[column(half), pl.ds(n * half_j, half_j)], relay.at[n], (hop_send, hop_recv), n,
            {"col": column(side)},
        )
        hop.start()
        hops.append(hop)

    def block(d):
        return pltpu.make_async_remote_copy(
            src_ref=p_ref.at[column(d)], dst_ref=window(col),
            send_sem=send.at[d], recv_sem=recv.at[inner, lax.rem(col, group)],
            device_id={"col": column(d), "inner": home(col)}, device_id_type=MESH,
        )

    mine = pltpu.make_async_copy(p_ref.at[col], window(col), own.at[0])
    others = [d for d in range(1, n_col) if d != half]
    for d in others:
        block(d).start()

    @pl.when(home(col) != inner)
    def _():
        block(0).start()

    @pl.when(home(col) == inner)
    def _():
        mine.start()

    z_copies = []
    for e in range(1, n_in):
        copy = remote(z_ref, zr.at[inner], (zsend, zrecv), e - 1, {"inner": lax.rem(inner + e, n_in)})
        copy.start()
        z_copies.append(copy)
    z_own = pltpu.make_async_copy(z_ref, zr.at[inner], own.at[1])
    z_own.start()

    ons = []
    for n, side in enumerate(sides):
        hops[n].wait_recv()
        source = column(-side)
        on = pltpu.make_async_remote_copy(
            src_ref=relay.at[n], dst_ref=window(source, n * half_j, half_j),
            send_sem=on_send.at[n], recv_sem=on_recv.at[n, inner],
            device_id={"col": column(half - side), "inner": home(source)}, device_id_type=MESH,
        )
        on.start()
        ons.append(on)

    for e in range(n_in):
        for g in range(group):
            source = inner * group + g
            tied = source == column(half)
            is_own = jnp.logical_and(inner == e, col == source)

            @pl.when(tied)
            def _(e=e):
                for n in range(2):
                    pltpu.make_async_remote_copy(
                        src_ref=relay.at[n], dst_ref=relay.at[n],
                        send_sem=on_send.at[n], recv_sem=on_recv.at[n, e],
                        device_id={"col": column(1), "inner": inner}, device_id_type=MESH,
                    ).wait_recv()

            @pl.when(jnp.logical_not(jnp.logical_or(tied, is_own)))
            def _(e=e, g=g):
                pltpu.make_async_remote_copy(
                    src_ref=p_ref.at[0], dst_ref=p_ref.at[0], send_sem=send.at[0], recv_sem=recv.at[e, g],
                    device_id={"col": column(1), "inner": inner}, device_id_type=MESH,
                ).wait_recv()

    @pl.when(home(col) == inner)
    def _():
        mine.wait()

    @pl.when(home(col) != inner)
    def _():
        block(0).wait_send()

    for d in others:
        block(d).wait_send()
    for copy in hops + ons:
        copy.wait_send()
    z_own.wait()
    for copy in z_copies:
        copy.wait()


def spread(p, z, sizes):
    n_row, n_col, n_in = sizes
    group = n_col // n_in
    own_j, slots, rank, cols = p.shape[1:]
    vmem = pl.BlockSpec(memory_space=pltpu.VMEM)
    return pl.pallas_call(
        functools.partial(spread_kernel, (n_col, n_in, group, own_j, cols)),
        out_shape=(
            jax.ShapeDtypeStruct((own_j, n_in, slots, rank, group * cols), p.dtype),
            jax.ShapeDtypeStruct((n_in,) + z.shape, z.dtype),
        ),
        in_specs=[vmem, vmem],
        out_specs=[vmem, vmem],
        scratch_shapes=[
            pltpu.VMEM((2, own_j // 2, slots, rank, cols), p.dtype),
            pltpu.SemaphoreType.DMA((n_col,)),
            pltpu.SemaphoreType.DMA((n_in, group)),
            pltpu.SemaphoreType.DMA((2,)),
            pltpu.SemaphoreType.DMA((2,)),
            pltpu.SemaphoreType.DMA((2,)),
            pltpu.SemaphoreType.DMA((2, n_in)),
            pltpu.SemaphoreType.DMA((n_in,)),
            pltpu.SemaphoreType.DMA((n_in,)),
            pltpu.SemaphoreType.DMA((2,)),
        ],
        compiler_params=pltpu.CompilerParams(collective_id=1, has_side_effects=True),
    )(p, z)


def factor_kernel(n_in, gram_ref, cross_ref, inv_ref, out_ref, gram_got, cross_got, send, recv, csend, crecv):
    inner = lax.axis_index("inner")
    peers = [lax.rem(inner + d, n_in) for d in range(1, n_in)]
    meet([{"inner": peer} for peer in peers])
    grams = [remote(gram_ref, gram_got.at[e], (send, recv), e, {"inner": p}) for e, p in enumerate(peers)]
    crosses = [remote(cross_ref, cross_got.at[e], (csend, crecv), e, {"inner": p}) for e, p in enumerate(peers)]
    for copy in grams + crosses:
        copy.start()
    for copy in grams:
        copy.wait()
    gram = gram_ref[...]
    for e in range(n_in - 1):
        gram = gram + gram_got[e]
    inverse_factor(gram, inv_ref)
    for copy in crosses:
        copy.wait()
    cross = cross_ref[...]
    for e in range(n_in - 1):
        cross = cross + cross_got[e]
    out_ref[...] = cross


def factor_over_inner(gram, cross, n_in):
    vmem = pl.BlockSpec(memory_space=pltpu.VMEM)
    return pl.pallas_call(
        functools.partial(factor_kernel, n_in),
        out_shape=(
            jax.ShapeDtypeStruct(gram.shape, gram.dtype),
            jax.ShapeDtypeStruct(cross.shape, cross.dtype),
        ),
        in_specs=[vmem, vmem],
        out_specs=[vmem, vmem],
        scratch_shapes=[
            pltpu.VMEM((n_in - 1,) + gram.shape, gram.dtype),
            pltpu.VMEM((n_in - 1,) + cross.shape, cross.dtype),
        ] + [pltpu.SemaphoreType.DMA((n_in - 1,))] * 4,
        compiler_params=pltpu.CompilerParams(collective_id=2, has_side_effects=True),
    )(gram, cross)


def inverse_factor(gram, out_ref):
    count, size, _ = gram.shape
    tall = lax.broadcasted_iota(jnp.int32, (size, size), 0)
    wide = lax.broadcasted_iota(jnp.int32, (size, size), 1)
    eye = (tall == wide).astype(WIDE)
    lines = lax.broadcasted_iota(jnp.int32, (8, 1), 0)
    works = []
    for j in range(count):
        full = jnp.concatenate([gram[j], eye], axis=1)
        works.append([full[8 * b : 8 * b + 8] for b in range(size // 8)])
    scales = [[] for _ in range(count)]
    for k in range(size):
        b0, in_b = k // 8, k % 8
        for j in range(count):
            work = works[j]
            line = work[b0][in_b : in_b + 1]
            pivot = line[:, k : k + 1]
            scales[j].append(lax.rsqrt(pivot))
            line = line * (1.0 / pivot)
            for b in range(b0, size // 8):
                column = work[b][:, k : k + 1]
                if b == b0:
                    if in_b == 7:
                        continue
                    column = jnp.where(lines > in_b, column, 0.0)
                work[b] = work[b] - column * line
    for j in range(count):
        scale = jnp.concatenate(scales[j], axis=0)
        out_ref[j] = jnp.concatenate(works[j], axis=0)[:, size:] * scale


def local(sizes, near_flags, row_factor, col_factor, near_block, inner_left, inner_right, sketch_matrix):
    n_row, n_col, n_in = sizes
    slots, own_j, rank, width = inner_left.shape
    js = own_j * rank
    total = width * n_row
    cols = total // n_col
    share = total // n_in
    xg, yg, yi, vg = gather_all(
        inner_left.reshape(slots, js, width), inner_right.reshape(slots, js, width), col_factor[0], sizes
    )
    nearness = near_flags[0]
    pieces = []
    for slot in range(slots):

        def lowrank(slot=slot):
            coupled = lax.dot_general(
                xg[slot], vg[slot], (((1,), (1,)), ((), ())), preferred_element_type=WIDE
            ).astype(NARROW)
            return jnp.dot(coupled, row_factor[0, slot], preferred_element_type=WIDE).astype(NARROW)

        def neardense(slot=slot):
            return jnp.dot(xg[slot], near_block[0, slot], preferred_element_type=WIDE).astype(NARROW)

        pieces.append(lax.cond(nearness[slot] > 0, neardense, lowrank))
    spread_out = jnp.stack([p.reshape(n_col, own_j, rank, cols) for p in pieces], axis=2)
    reduced = jnp.einsum(
        "kjrl,jsl->krjs", yg.reshape(slots, own_j, rank, total), sketch_matrix, preferred_element_type=WIDE
    ).astype(NARROW)
    got, reduced_all = spread(spread_out, reduced.reshape(slots * rank, js), sizes)
    stacked = got.reshape(own_j, n_in * slots * rank, share)
    z_all = reduced_all.reshape(n_in * slots * rank, own_j, rank)
    sampled = jnp.einsum("ajs,jal->jsl", z_all, stacked, preferred_element_type=WIDE)
    high = sampled.astype(NARROW)
    low = (sampled - high.astype(WIDE)).astype(NARROW)
    both = jnp.concatenate([high, low], axis=1)
    cross = jnp.einsum("jsl,jal->jsa", both, stacked, preferred_element_type=WIDE)
    cross = cross[:, :rank] + cross[:, rank:]
    gram = jnp.einsum("jsl,jtl->jst", sampled, sampled, precision=HIGHEST) / total
    inverse, cross = factor_over_inner(gram, cross, n_in)
    basis = jnp.einsum("jst,jtl->jsl", inverse, sampled, precision=HIGHEST)
    projected = jnp.einsum("jst,jta->jsa", inverse, cross, precision=HIGHEST) / math.sqrt(total)
    p_high = projected.astype(NARROW)
    p_low = (projected - p_high.astype(WIDE)).astype(NARROW)
    yk = yi.reshape(n_in * slots, own_j, rank, share)
    p_both = jnp.concatenate([p_high, p_low], axis=1).reshape(own_j, 2 * rank, n_in * slots, rank)
    coupling = jnp.einsum("jskr,kjrl->jsl", p_both, yk, preferred_element_type=WIDE)
    coupling = coupling[:, :rank] + coupling[:, rank:]
    return (basis[None], coupling[None])


def solution(mesh):
    sizes = (mesh.shape["row"], mesh.shape["col"], mesh.shape["inner"])
    in_specs = (
        P("row", "inner"),
        P("row", "inner", None, "col"),
        P("row", "inner", None, "col"),
        P("row", "inner", None, "col"),
        P("inner", "col", None, "row"),
        P("inner", "col", None, "row"),
        P("col", None, None),
    )
    out_specs = (P("row", "col", None, "inner"), P("row", "col", None, "inner"))
    return jax.shard_map(
        functools.partial(local, sizes), mesh=mesh, in_specs=in_specs, out_specs=out_specs, check_vma=False
    )
```

profile of v0, /device:TPU:0, one launch (start us, length us, event | category | flops | bytes accessed | tf_op | source)
XLA Modules:
  0.0 258.6 jit_solution(200051847825452977)
XLA Ops:
  0.6 0.0 copy-start
  0.6 1.4 fusion.92
  4.0 123.6 %shard_map.86 = (bf16[3,1024,2048]{2,1,0:T(8,128)(2,1)}, bf16[3,256,2048]{2,1,0:T(8,128)(2,1)}, bf16[2,3,256,1024]{3,2,1,0:T(8,128)(2,1)}, bf16[3,64,2048]{2,1,0:T(8,128)(2,1)}) custom-call(bf16[3,256,512]{2,1,0:T(8,128)(2,1)} %bitcast.130, bf16[3,256,512]{2,1,0:T(8,128)(2,1)} %bitcast.131, bf16[3,64,512]{2,1,0:T(8,128)(2,1)} %bitcast.132), custom_call_target="tpu_custom_call" | custom-call | tf_op jit(solution)/shard_map/pallas_call | solution.py:160
  127.6 0.0 copy-done
  127.6 0.0 copy-start.2
  127.6 2.9 %fusion.82 = bf16[3,64,4,64]{3,1,0,2:T(8,128)(2,1)S(1)} fusion(bf16[3,4,64,2048]{3,2,1,0:T(8,128)(2,1)} %bitcast.133, bf16[4,64,2048]{2,1,0:T(8,128)(2,1)S(1)} %copy-done), kind=kOutput, calls=%fused_computation.54 | convolution fusion | flops 201375744 | bytes 4292608 | tf_op jit(solution)/shard_map/kjrl,jsl->krjs/dot_general | solution.py:413
  130.5 0.2 copy.21
  130.7 0.8 reshape.49.z_ref
  131.5 0.0 copy-done.2
  131.5 4.1 %conditional.5 = (bf16[4,4,1,64,512]{4,3,1,0,2:T(8,128)(2,1)S(1)}) conditional(s32[]{:T(128)} %bitcast.28, (bf16[3,1024,2048]{2,1,0:T(8,128)(2,1)}, bf16[3,64,2048]{2,1,0:T(8,128)(2,1)}, bf16[1,3,64,512]{3,2,1,0:T(8,128)(2,1)S(1)}) %tuple.46, (bf16[3,1024,2048]{2,1,0:T(8,128)(2,1)}, bf16[1,3,2048,512]{3,2,1,0:T(8,128)(2,1)}) %tuple.33), branch_computations={%region_4.0_spmd, %region_5.0_spmd} | conditional | flops 2148007936 | bytes 7340040 | solution.py:411
  131.5 4.1 %convolution_convert_fusion.2 = bf16[1024,512]{1,0:T(8,128)(2,1)S(1)} fusion(bf16[3,1024,2048]{2,1,0:T(8,128)(2,1)} %get-tuple-element.52, bf16[3,64,2048]{2,1,0:T(8,128)(2,1)} %get-tuple-element.53, bf16[1,3,64,512]{3,2,1,0:T(8,128)(2,1)S(1)} %get-tuple-element.54), kind=kOutput, calls=%fused_computation.33 | convolution fusion | flops 336134144 | bytes 5570560 | tf_op jit(solution)/shard_map/cond/branch_0_fun/dot_general | solution.py:406
  135.6 4.1 %conditional.4 = (bf16[4,4,1,64,512]{4,3,1,0,2:T(8,128)(2,1)S(1)}) conditional(s32[]{:T(128)} %bitcast.26, (bf16[3,1024,2048]{2,1,0:T(8,128)(2,1)}, bf16[3,64,2048]{2,1,0:T(8,128)(2,1)}, bf16[1,3,64,512]{3,2,1,0:T(8,128)(2,1)S(1)}) %tuple.47, (bf16[3,1024,2048]{2,1,0:T(8,128)(2,1)}, bf16[1,3,2048,512]{3,2,1,0:T(8,128)(2,1)}) %tuple.33), branch_computations={%region_2.0_spmd, %region_3.0_spmd} | conditional | flops 2148007936 | bytes 7340040 | solution.py:411
  135.6 4.1 %convolution_convert_fusion.1 = bf16[1024,512]{1,0:T(8,128)(2,1)S(1)} fusion(bf16[3,1024,2048]{2,1,0:T(8,128)(2,1)} %get-tuple-element.47, bf16[3,64,2048]{2,1,0:T(8,128)(2,1)} %get-tuple-element.48, bf16[1,3,64,512]{3,2,1,0:T(8,128)(2,1)S(1)} %get-tuple-element.49), kind=kOutput, calls=%fused_computation.18 | convolution fusion | flops 336134144 | bytes 5570560 | tf_op jit(solution)/shard_map/cond/branch_0_fun/dot_general | solution.py:406
  139.8 6.2 %conditional.3 = (bf16[4,4,1,64,512]{4,3,1,0,2:T(8,128)(2,1)}) conditional(s32[]{:T(128)} %bitcast.21, (bf16[3,1024,2048]{2,1,0:T(8,128)(2,1)}, bf16[3,64,2048]{2,1,0:T(8,128)(2,1)}, bf16[1,3,64,512]{3,2,1,0:T(8,128)(2,1)S(1)}) %tuple.48, (bf16[3,1024,2048]{2,1,0:T(8,128)(2,1)}, bf16[1,3,2048,512]{3,2,1,0:T(8,128)(2,1)}) %tuple.33), branch_computations={%region_0.0_spmd, %region_1.0_spmd} | conditional | flops 2148007936 | bytes 7340040 | solution.py:411
  139.8 6.2 %fusion.19 = bf16[1024,512]{1,0:T(8,128)(2,1)} fusion(bf16[1,3,2048,512]{3,2,1,0:T(8,128)(2,1)} %get-tuple-element.46, bf16[3,1024,2048]{2,1,0:T(8,128)(2,1)} %get-tuple-element.45), kind=kOutput, calls=%fused_computation.14 | convolution fusion | flops 2148007936 | bytes 7340032 | tf_op jit(solution)/shard_map/cond/branch_1_fun/dot_general | solution.py:409
  146.0 3.2 %pad_maximum_fusion.p_ref = bf16[4,4,3,64,512]{4,3,2,1,0:T(8,128)(2,1)} fusion(bf16[4,4,1,64,512]{4,3,2,1,0:T(8,128)(2,1)S(1)} %bitcast.123, bf16[4,4,1,64,512]{4,3,2,1,0:T(8,128)(2,1)S(1)} %bitcast.126, bf16[4,4,1,64,512]{4,3,2,1,0:T(8,128)(2,1)} %bitcast.129), kind=kLoop, calls=%fused_computation.45 | loop fusion | flops 3145728 | bytes 6291456 | tf_op jit(solution)/shard_map/stack | solution.py:412
  149.2 76.8 %shard_map.87 = (bf16[4,2,3,64,1024]{4,3,2,1,0:T(8,128)(2,1)}, bf16[2,192,256]{2,1,0:T(8,128)(2,1)}) custom-call(bf16[4,4,3,64,512]{4,3,2,1,0:T(8,128)(2,1)} %pad_maximum_fusion.p_ref, bf16[192,256]{1,0:T(8,128)(2,1)} %reshape.49.z_ref), custom_call_target="tpu_custom_call" | custom-call | tf_op jit(solution)/shard_map/pallas_call | solution.py:293
  226.0 1.1 copy.22
  227.1 0.2 reshape.50
  227.3 0.0 copy-start.1
  227.3 2.7 %subtract_convert_fusion = (bf16[4,64,1024]{2,1,0:T(8,128)(2,1)S(1)}, bf16[4,64,1024]{2,1,0:T(8,128)(2,1)S(1)}, f32[4,64,1024]{2,1,0:T(8,128)S(1)}) fusion(bf16[384,4,64]{0,2,1:T(8,128)(2,1)S(1)} %reshape.50, bf16[4,384,1024]{2,1,0:T(8,128)(2,1)} %bitcast.117), kind=kOutput, calls=%fused_computation.63 | convolution fusion | flops 202375168 | bytes 5439488 | tf_op jit(solution)/shard_map/ajs,jal->jsl/dot_general | solution.py:419
  230.0 0.1 copy-done.1
  230.1 1.1 fusion.86
  231.2 0.8 slice_add_fusion.1.cross_ref
  232.0 1.7 convolution_multiply_fusion.1.gram_ref
  233.7 16.3 %shard_map.88 = (f32[4,64,64]{2,1,0:T(8,128)}, f32[4,64,384]{2,1,0:T(8,128)}) custom-call(f32[4,64,64]{2,1,0:T(8,128)} %convolution_multiply_fusion.1.gram_ref, f32[4,64,384]{2,1,0:T(8,128)} %slice_add_fusion.1.cross_ref), custom_call_target="tpu_custom_call" | custom-call | tf_op jit(solution)/shard_map/pallas_call | solution.py:341
  250.1 2.9 %convolution_bitcast_fusion = f32[1,4,64,1024]{3,2,1,0:T(8,128)} fusion(f32[4,64,64]{2,1,0:T(8,128)} %get-tuple-element.72, f32[4,64,1024]{2,1,0:T(8,128)S(1)} %get-tuple-element.82), kind=kOutput, calls=%fused_computation.51 | convolution fusion | flops 201326592 | bytes 2162688 | tf_op jit(solution)/shard_map/jst,jtl->jsl/dot_general | solution.py:427
  253.0 1.5 subtract_convert_fusion.1
  254.6 0.2 copy.23
  254.8 2.7 %fusion.76 = f32[4,128,1024]{2,1,0:T(8,128)S(1)} fusion(bf16[4,128,6,64]{1,3,2,0:T(8,128)(2,1)S(1)} %bitcast.120, bf16[6,4,64,1024]{3,2,1,0:T(8,128)(2,1)} %bitcast.119), kind=kOutput, calls=%fused_computation.50 | convolution fusion | flops 402653184 | bytes 5636096 | tf_op jit(solution)/shard_map/jskr,kjrl->jsl/dot_general | solution.py:433
  257.4 1.1 fusion.85
  (1 shorter events, 0.0 us)
Async XLA Ops:
  0.6 127.0 %copy-start = (bf16[4,64,2048]{2,1,0:T(8,128)(2,1)S(1)}, bf16[4,64,2048]{2,1,0:T(8,128)(2,1)}, u32[]{:S(2)}) copy-start(bf16[4,64,2048]{2,1,0:T(8,128)(2,1)} %param.19) | copy-start | bytes 3145732
  127.6 3.9 %copy-start.2 = (bf16[1,3,64,512]{3,2,1,0:T(8,128)(2,1)S(1)}, bf16[1,3,64,512]{3,2,1,0:T(8,128)(2,1)}, u32[]{:S(2)}) copy-start(bf16[1,3,64,512]{3,2,1,0:T(8,128)(2,1)} %param.14) | copy-start | bytes 589828
  227.3 2.8 %copy-start.1 = (bf16[4,2,3,64,1024]{4,3,2,1,0:T(8,128)(2,1)S(1)}, bf16[4,2,3,64,1024]{4,3,2,1,0:T(8,128)(2,1)}, u32[]{:S(2)}) copy-start(bf16[4,2,3,64,1024]{4,3,2,1,0:T(8,128)(2,1)} %get-tuple-element.71) | copy-start | bytes 9437188
where the time goes:
time: 259 us
  Pallas kernels  217 us (84%)
  matrix products  29.9 us (12%)
  other arithmetic  5.14 us (2%)
  local copies, waits for them, and re-layouts  4.01 us (2%)
  between operations  2.71 us (1%)
    pallas_call x1, Pallas kernels, gather_all(): pl.pallas_call(functools.partial(gather_kernel, dims), out_shape=(jax.Sha...  124 us
    pallas_call x1, Pallas kernels, spread(): pl.pallas_call(functools.partial(spread_kernel, (n_col, n_in, group, own_...  76.8 us
    pallas_call x1, Pallas kernels, factor_over_inner(): pl.pallas_call(functools.partial(factor_kernel, n_in), out_shape=(jax.Sha...  16.3 us
    dot_general x2, matrix products, lowrank(): jnp.dot(coupled, row_factor[0, slot], preferred_element_type=WIDE)  8.22 us
    dot_general x1, matrix products, neardense(): jnp.dot(xg[slot], near_block[0, slot], preferred_element_type=WIDE)  6.16 us

commit v1 on v0

v1 whole, which is shorter than its diff:
```python
import functools
import math

import jax
import jax.numpy as jnp
from jax import lax
from jax.experimental import pallas as pl
from jax.experimental.pallas import tpu as pltpu
from jax.sharding import PartitionSpec as P

MESH = pl.DeviceIdType.MESH
HIGHEST = lax.Precision.HIGHEST
WIDE = jnp.float32
NARROW = jnp.bfloat16
NT = (((1,), (1,)), ((), ()))
TN = (((0,), (0,)), ((), ()))


def remote(src, dst, send, recv, device):
    return pltpu.make_async_remote_copy(
        src_ref=src, dst_ref=dst, send_sem=send, recv_sem=recv, device_id=device, device_id_type=MESH
    )


def meet(devices):
    barrier = pltpu.get_barrier_semaphore()
    for device in devices:
        pl.semaphore_signal(barrier, inc=1, device_id=device, device_id_type=MESH)
    pl.semaphore_wait(barrier, len(devices))


def split(value):
    high = value.astype(NARROW)
    return high, (value - high.astype(WIDE)).astype(NARROW)


def lanes(length):
    return -(-length // 128) * 128


def product_kernel(
    dims, mask_ref, u_ref, v_ref, d_ref, x_ref, y_ref, o_ref,
    s_home, cross_out, gram_out, yg,
    xg, vg, deff, pbuf, zt, zpart, zgot, zown, spart, ssend, sgot, msend, mgot, hsend,
    x_z_send, x_z_recv, x_f_send, x_f_recv, x_t_send, x_t_recv,
    v_send, v_recv, z_z_send, z_z_recv, z_f_send, z_f_recv, z_t_send, z_t_recv, zp_send, zp_recv,
    s_send, s_recv, m_send, m_recv, h_send, h_recv, y_f_send, y_f_recv, y_t_send, y_t_recv, own,
):
    n_row, n_col, n_in, slots, own_j, rank, width, cols = dims
    js = own_j * rank
    kr = slots * rank
    group = n_col // n_in
    planes = n_row // 2
    zrows = js // n_row
    row, col, inner = lax.axis_index("row"), lax.axis_index("col"), lax.axis_index("inner")
    plane = lax.div(row, 2)
    parity = lax.rem(row, 2)
    twin = {"row": row + 1 - 2 * parity}
    far_planes = [lax.rem(plane + f, planes) for f in range(1, planes)]
    back_planes = [lax.rem(plane + planes - f, planes) for f in range(1, planes)]
    fars = [{"row": 2 * p + parity} for p in far_planes]
    up, down = {"col": lax.rem(col + 1, n_col)}, {"col": lax.rem(col + n_col - 1, n_col)}
    has_up, has_down = col < n_col - 1, col > 0
    row_peers = [lax.rem(row + d, n_row) for d in range(1, n_row)]
    in_peers = [lax.rem(inner + e, n_in) for e in range(1, n_in)]
    home = lax.div(col, group)
    home_lane = pl.multiple_of(lax.rem(col, group) * cols, cols)
    total = 2 * slots * 0 + n_row * width

    meet(
        [{"row": r} for r in row_peers]
        + [{"col": lax.rem(col + d, n_col)} for d in range(1, n_col)]
        + [{"inner": p} for p in in_peers]
    )

    def at_rows(s):
        return pl.ds(pl.multiple_of(s * js, js), js)

    def x_at(s, k, p, q):
        return xg.at[k, at_rows(s), pl.ds(pl.multiple_of((2 * p + q) * width, width), width)]

    def v_at(s):
        return vg.at[:, :, pl.ds(pl.multiple_of(s * cols, cols), cols)]

    def z_at(s, p, q):
        return zt.at[s, pl.ds(pl.multiple_of((2 * p + q) * zrows, zrows), zrows)]

    def y_at(p, q):
        return yg.at[:, :, pl.ds(pl.multiple_of((2 * p + q) * width, width), width)]

    def x_line(s, k, way, src=None):
        place = x_at(s, k, plane, parity)
        return remote(
            place if src is None else src, place, x_z_send.at[way, s, k], x_z_recv.at[s, k], (up, down)[way]
        )

    def x_far(s, k, f, src=None):
        place = x_at(s, k, plane, parity)
        return remote(place if src is None else src, place, x_f_send.at[f, s, k], x_f_recv.at[f, s, k], fars[f])

    def x_twin(s, k, p, src=None):
        place = x_at(s, k, p, parity)
        return remote(place if src is None else src, place, x_t_send.at[p, s, k], x_t_recv.at[p, s, k], twin)

    def z_line(s, way, src=None):
        place = z_at(s, plane, parity)
        return remote(place if src is None else src, place, z_z_send.at[way, s], z_z_recv.at[s], (up, down)[way])

    def z_far(s, f, src=None):
        place = z_at(s, plane, parity)
        return remote(place if src is None else src, place, z_f_send.at[f, s], z_f_recv.at[f, s], fars[f])

    def z_twin(s, p, src=None):
        place = z_at(s, p, parity)
        return remote(place if src is None else src, place, z_t_send.at[p, s], z_t_recv.at[p, s], twin)

    def v_line(s, way, src=None):
        return remote(
            v_at(s) if src is None else src, v_at(s), v_send.at[way, s], v_recv.at[s], (up, down)[way]
        )

    def z_piece(d):
        rows = pl.ds(pl.multiple_of(row_peers[d] * zrows, zrows), zrows)
        return remote(zpart.at[rows], zgot.at[d], zp_send.at[d], zp_recv.at[d], {"row": row_peers[d]})

    def y_far(f):
        return remote(y_ref, y_at(plane, parity), y_f_send.at[f], y_f_recv.at[f], fars[f])

    def y_twin(p, src=None):
        place = y_at(p, parity)
        return remote(place if src is None else src, place, y_t_send.at[p], y_t_recv.at[p], twin)

    def s_peer(s, e):
        return remote(ssend.at[s], sgot.at[e, s], s_send.at[e, s], s_recv.at[e, s], {"inner": in_peers[e]})

    def m_home(s, source):
        return remote(msend.at[s], mgot.at[source], m_send.at[s], m_recv.at[source], {"col": s})

    def h_home(s, source):
        lane = pl.multiple_of(lax.rem(source, group) * cols, cols)
        return remote(
            hsend.at[s], s_home.at[:, pl.ds(lane, cols)], h_send.at[s], h_recv.at[lax.rem(source, group)], {"col": s}
        )

    def unit(b):
        both = jnp.minimum(col, n_col - 1 - col)
        near = lax.div(b + 1, 2)
        paired = jnp.where(lax.rem(b, 2) == 1, col - near, col + near)
        single = jnp.where(col < n_col - 1 - col, col + (b - both), col - (b - both))
        return jnp.where(b <= 2 * both, paired, single)

    fetches = [pltpu.make_async_copy(d_ref.at[k], deff.at[k], own.at[k]) for k in range(slots)]
    for fetch in fetches:
        fetch.start()

    @pl.when(has_up)
    def _():
        v_line(col, 0, v_ref).start()

    @pl.when(has_down)
    def _():
        v_line(col, 1, v_ref).start()

    for f in range(planes - 1):
        x_far(col, 0, f, x_ref.at[0]).start()
    for k in range(slots):
        x_twin(col, k, plane, x_ref.at[k]).start()
    y_twin(plane, y_ref).start()

    omega_at = pl.ds(pl.multiple_of(row * width, width), width)
    for j in range(own_j):
        inner_rows = jnp.concatenate([y_ref[k, j * rank : (j + 1) * rank] for k in range(slots)], axis=0)
        part = lax.dot_general(o_ref[j, :, omega_at], inner_rows, NT, preferred_element_type=WIDE)
        zpart[j * rank : (j + 1) * rank, 0:kr] = part
    for k in range(slots):
        xg[k, at_rows(col), pl.ds(pl.multiple_of(row * width, width), width)] = x_ref[k]
    vg[:, :, pl.ds(pl.multiple_of(col * cols, cols), cols)] = v_ref[...]
    yg[:, :, pl.ds(pl.multiple_of(row * width, width), width)] = y_ref[...]
    for d in range(n_row - 1):
        z_piece(d).start()
    for k in range(1, slots):
        for f in range(planes - 1):
            x_far(col, k, f, x_ref.at[k]).start()

    for t in range(1, n_col):

        @pl.when(col >= t)
        def _(t=t):
            v_line(col - t, 0).wait_recv()

            @pl.when(has_up)
            def _():
                v_line(col - t, 0).start()

        @pl.when(col + t < n_col)
        def _(t=t):
            v_line(col + t, 1).wait_recv()

            @pl.when(has_down)
            def _():
                v_line(col + t, 1).start()

    total_z = zpart[pl.ds(pl.multiple_of(row * zrows, zrows), zrows), 0:kr]
    for d in range(n_row - 1):
        z_piece(d).wait_recv()
        total_z = total_z + zgot[d, :, 0:kr]
    quarter = total_z.astype(NARROW)
    zown[:, 0:kr] = quarter
    zt[col, pl.ds(pl.multiple_of(row * zrows, zrows), zrows), 0:kr] = quarter

    @pl.when(has_up)
    def _():
        for k in range(slots):
            x_line(col, k, 0, x_ref.at[k]).start()
            if k == 0:
                z_line(col, 0, zown).start()

    @pl.when(has_down)
    def _():
        for k in range(slots):
            x_line(col, k, 1, x_ref.at[k]).start()
            if k == 0:
                z_line(col, 1, zown).start()

    for f in range(planes - 1):
        z_far(col, f, zown).start()
    z_twin(col, plane, zown).start()

    step_rows = min(512, total)
    for k in range(slots):
        fetches[k].wait()

        def effective(i, carry, k=k):
            at = pl.ds(pl.multiple_of(i * step_rows, step_rows), step_rows)
            low = lax.dot_general(vg[k, :, at], u_ref[k], TN, preferred_element_type=WIDE)
            dense = deff[k, at, :].astype(WIDE)
            deff[k, at, :] = jnp.where(mask_ref[k, 0:1, :] > 0.5, dense, low).astype(NARROW)
            return carry

        lax.fori_loop(0, total // step_rows, effective, 0)

    def pump(b, k):
        for side in range(2):
            s = col - (b + 1) if side == 0 else col + (b + 1)
            valid = s >= 0 if side == 0 else s < n_col

            @pl.when(valid)
            def _(s=s, side=side):
                x_line(s, k, side).wait_recv()

                @pl.when((has_up, has_down)[side])
                def _():
                    x_line(s, k, side).start()

                for f in range(planes - 1):
                    x_far(s, k, f).start()
                x_twin(s, k, plane).start()

                @pl.when(k == 0)
                def _():
                    z_line(s, side).wait_recv()

                    @pl.when((has_up, has_down)[side])
                    def _():
                        z_line(s, side).start()

                    for f in range(planes - 1):
                        z_far(s, f).start()
                    z_twin(s, plane).start()

        here = unit(b)
        for f in range(planes - 1):
            x_far(here, k, f).wait_recv()
            x_twin(here, k, back_planes[f]).start()

        @pl.when(k == 0)
        def _():
            for f in range(planes - 1):
                z_far(here, f).wait_recv()
                z_twin(here, back_planes[f]).start()

    def piece(b, k):
        s = unit(b)
        for p in range(planes):
            x_twin(s, k, p).wait_recv()
        out = jnp.dot(xg[k, at_rows(s), :], deff[k], preferred_element_type=WIDE).astype(NARROW)
        for j in range(own_j):
            pbuf[s, j, pl.ds(pl.multiple_of(k * rank, rank), rank), :] = out[j * rank : (j + 1) * rank]

    def sample(b):
        s = unit(b)
        for p in range(planes):
            z_twin(s, p).wait_recv()
        for j in range(own_j):
            rows = slice(j * rank, (j + 1) * rank)
            part = jnp.dot(zt[s, rows, 0:kr], pbuf[s, j], preferred_element_type=WIDE)
            spart[s, rows, :] = part
            ssend[s, rows, :] = part.astype(NARROW)
        for e in range(n_in - 1):
            s_peer(s, e).start()

    def finish(b):
        s = unit(b)
        for e in range(n_in - 1):
            s_peer(s, e).wait_recv()
        for j in range(own_j):
            rows = slice(j * rank, (j + 1) * rank)
            whole = spart[s, rows, :]
            for e in range(n_in - 1):
                whole = whole + sgot[e, s, rows, :].astype(WIDE)
            high, low = split(whole)
            hsend[s, rows, :] = high
            left = jnp.concatenate([high, low], axis=0)
            right = jnp.concatenate([pbuf[s, j], left], axis=0)
            both = lax.dot_general(left, right, NT, preferred_element_type=WIDE)
            top, low_part = both[:rank], both[rank:]
            cross = top[:, :kr] + low_part[:, :kr]
            gram = top[:, kr : kr + rank] + top[:, kr + rank :] + low_part[:, kr : kr + rank]
            gram_high, gram_low = split(gram)
            msend[s, rows, 0:kr] = cross.astype(NARROW)
            msend[s, rows, kr : kr + rank] = gram_high
            msend[s, rows, kr + rank : kr + 2 * rank] = gram_low

        @pl.when(s != col)
        def _():
            m_home(s, col).start()

            @pl.when(home == inner)
            def _():
                h_home(s, col).start()

        @pl.when(s == col)
        def _():
            mgot[col] = msend[s]

            @pl.when(home == inner)
            def _():
                s_home[:, pl.ds(home_lane, cols)] = hsend[s]

    count = n_col * slots

    def step(q, carry):
        @pl.when(q < count)
        def _():
            pump(lax.div(q, slots), lax.rem(q, slots))

        @pl.when(q == (n_col - 1) * slots)
        def _():
            for f in range(planes - 1):
                y_far(f).start()

        @pl.when(q > 0)
        def _():
            last = q - 1
            b, k = lax.div(last, slots), lax.rem(last, slots)
            piece(b, k)

            @pl.when(k == slots - 1)
            def _():
                sample(b)

                @pl.when(b > 0)
                def _():
                    finish(b - 1)

        return carry

    lax.fori_loop(0, count + 1, step, 0)
    finish(n_col - 1)

    for f in range(planes - 1):
        y_far(f).wait_recv()
        y_twin(back_planes[f]).start()
    for d in range(1, n_col):
        source = lax.rem(col + d, n_col)
        m_home(source, source).wait_recv()
    for g in range(group):
        source = inner * group + g

        @pl.when(source != col)
        def _(source=source):
            h_home(source, source).wait_recv()

    crosses = mgot[0, :, 0:kr].astype(WIDE)
    grams = mgot[0, :, kr : kr + rank].astype(WIDE) + mgot[0, :, kr + rank : kr + 2 * rank].astype(WIDE)
    for c in range(1, n_col):
        crosses = crosses + mgot[c, :, 0:kr].astype(WIDE)
        grams = grams + mgot[c, :, kr : kr + rank].astype(WIDE)
        grams = grams + mgot[c, :, kr + rank : kr + 2 * rank].astype(WIDE)
    cross_out[:, 0:kr] = crosses
    gram_out[...] = grams.reshape(own_j, rank, rank) * (1.0 / total)

    for p in range(planes):
        y_twin(p).wait_recv()
        y_twin(p).wait_send()
    for f in range(planes - 1):
        y_far(f).wait_send()
    for d in range(n_row - 1):
        z_piece(d).wait_send()

    def drain(s, carry):
        @pl.when(jnp.logical_and(has_up, s <= col))
        def _():
            v_line(s, 0).wait_send()
            z_line(s, 0).wait_send()
            for k in range(slots):
                x_line(s, k, 0).wait_send()

        @pl.when(jnp.logical_and(has_down, s >= col))
        def _():
            v_line(s, 1).wait_send()
            z_line(s, 1).wait_send()
            for k in range(slots):
                x_line(s, k, 1).wait_send()

        for f in range(planes - 1):
            z_far(s, f).wait_send()
            for k in range(slots):
                x_far(s, k, f).wait_send()
        for p in range(planes):
            z_twin(s, p).wait_send()
            for k in range(slots):
                x_twin(s, k, p).wait_send()
        for e in range(n_in - 1):
            s_peer(s, e).wait_send()

        @pl.when(s != col)
        def _():
            m_home(s, col).wait_send()

            @pl.when(home == inner)
            def _():
                h_home(s, col).wait_send()

        return carry

    lax.fori_loop(0, n_col, drain, 0)


def product(mask, u, v, d, x, y, omega, sizes):
    n_row, n_col, n_in = sizes
    slots, js, width = x.shape
    own_j, rank, total = omega.shape
    cols = u.shape[-1]
    planes = n_row // 2
    kr = slots * rank
    group = n_col // n_in
    share = total // n_in
    vmem = pl.BlockSpec(memory_space=pltpu.VMEM)
    dma = pltpu.SemaphoreType.DMA
    dims = (n_row, n_col, n_in, slots, own_j, rank, width, cols)
    return pl.pallas_call(
        functools.partial(product_kernel, dims),
        out_shape=(
            jax.ShapeDtypeStruct((js, share), NARROW),
            jax.ShapeDtypeStruct((js, lanes(kr)), WIDE),
            jax.ShapeDtypeStruct((own_j, rank, rank), WIDE),
            jax.ShapeDtypeStruct((slots, js, total), NARROW),
        ),
        in_specs=[vmem, vmem, vmem, pl.BlockSpec(memory_space=pltpu.HBM), vmem, vmem, vmem],
        out_specs=[vmem] * 4,
        scratch_shapes=[
            pltpu.VMEM((slots, n_col * js, total), NARROW),
            pltpu.VMEM((slots, rank, total), NARROW),
            pltpu.VMEM((slots, total, cols), NARROW),
            pltpu.VMEM((n_col, own_j, kr, cols), NARROW),
            pltpu.VMEM((n_col, js, lanes(kr)), NARROW),
            pltpu.VMEM((js, lanes(kr)), WIDE),
            pltpu.VMEM((n_row - 1, js // n_row, lanes(kr)), WIDE),
            pltpu.VMEM((js // n_row, lanes(kr)), NARROW),
            pltpu.VMEM((n_col, js, cols), WIDE),
            pltpu.VMEM((n_col, js, cols), NARROW),
            pltpu.VMEM((n_in - 1, n_col, js, cols), NARROW),
            pltpu.VMEM((n_col, js, lanes(kr + 2 * rank)), NARROW),
            pltpu.VMEM((n_col, js, lanes(kr + 2 * rank)), NARROW),
            pltpu.VMEM((n_col, js, cols), NARROW),
            dma((2, n_col, slots)), dma((n_col, slots)),
            dma((planes - 1, n_col, slots)), dma((planes - 1, n_col, slots)),
            dma((planes, n_col, slots)), dma((planes, n_col, slots)),
            dma((2, n_col)), dma((n_col,)),
            dma((2, n_col)), dma((n_col,)),
            dma((planes - 1, n_col)), dma((planes - 1, n_col)),
            dma((planes, n_col)), dma((planes, n_col)),
            dma((n_row - 1,)), dma((n_row - 1,)),
            dma((n_in - 1, n_col)), dma((n_in - 1, n_col)),
            dma((n_col,)), dma((n_col,)),
            dma((n_col,)), dma((group,)),
            dma((planes - 1,)), dma((planes - 1,)),
            dma((planes,)), dma((planes,)),
            dma((slots,)),
        ],
        compiler_params=pltpu.CompilerParams(
            collective_id=0, has_side_effects=True, vmem_limit_bytes=60 * 1024 * 1024
        ),
    )(mask, u, v, d, x, y, omega)


def factor_kernel(
    dims, s_ref, cross_ref, gram_ref, yg_ref, basis_ref, coupling_ref,
    inv, cross_got, yb, c_send, c_recv, y_send, y_recv, t_send, t_recv,
):
    n_in, slots, own_j, rank, share = dims
    half = own_j * rank // 2
    kr = slots * rank
    row, inner = lax.axis_index("row"), lax.axis_index("inner")
    parity = lax.rem(row, 2)
    twin = {"row": row + 1 - 2 * parity}
    peers = [lax.rem(inner + e, n_in) for e in range(1, n_in)]
    meet([twin] + [{"inner": peer} for peer in peers])
    mine = pl.ds(pl.multiple_of(parity * half, half), half)
    crosses, halves, passed = [], [], []
    for e, peer in enumerate(peers):
        there = {"inner": peer}
        lane = pl.ds(pl.multiple_of(peer * share, share), share)
        crosses.append(remote(cross_ref, cross_got.at[e], c_send.at[e], c_recv.at[e], there))
        halves.append(
            remote(yg_ref.at[:, mine, lane], yb.at[e, :, mine], y_send.at[e], y_recv.at[e], there)
        )
        passed.append(remote(yb.at[e, :, mine], yb.at[e, :, mine], t_send.at[e], t_recv.at[e], twin))
    for copy in crosses + halves:
        copy.start()
    inverse_factor(gram_ref[...], inv)
    for e in range(n_in - 1):
        halves[e].wait_recv()
        passed[e].start()
    for copy in crosses:
        copy.wait()
    scale = 1.0 / math.sqrt(share * n_in)
    lane = pl.ds(pl.multiple_of(inner * share, share), share)
    left = []
    for j in range(own_j):
        rows = slice(j * rank, (j + 1) * rank)
        high, low = split(inv[j])
        both = jnp.concatenate([high, low], axis=0)
        out = jnp.dot(both, s_ref[rows, :], preferred_element_type=WIDE)
        basis_ref[j] = out[:rank] + out[rank:]
        crossed = jnp.concatenate(
            [cross_ref[rows, 0:kr]] + [cross_got[e, rows, 0:kr] for e in range(n_in - 1)], axis=1
        )
        projected = jnp.dot(inv[j], crossed, precision=HIGHEST, preferred_element_type=WIDE) * scale
        left.append(jnp.concatenate(split(projected), axis=0))
    for copy in passed:
        copy.wait_recv()
    for j in range(own_j):
        rows = slice(j * rank, (j + 1) * rank)
        right = [yg_ref[k, rows, lane] for k in range(slots)]
        right += [yb[e, k, rows, :] for e in range(n_in - 1) for k in range(slots)]
        out = jnp.dot(left[j], jnp.concatenate(right, axis=0), preferred_element_type=WIDE)
        coupling_ref[j] = out[:rank] + out[rank:]
    for copy in halves + passed:
        copy.wait_send()


def factor(s_home, cross, gram, yg, n_in):
    slots, js, total = yg.shape
    own_j, rank, _ = gram.shape
    share = total // n_in
    vmem = pl.BlockSpec(memory_space=pltpu.VMEM)
    dma = pltpu.SemaphoreType.DMA((n_in - 1,))
    out = jax.ShapeDtypeStruct((own_j, rank, share), WIDE)
    return pl.pallas_call(
        functools.partial(factor_kernel, (n_in, slots, own_j, rank, share)),
        out_shape=(out, out),
        in_specs=[vmem] * 4,
        out_specs=[vmem] * 2,
        scratch_shapes=[
            pltpu.VMEM(gram.shape, WIDE),
            pltpu.VMEM((n_in - 1,) + cross.shape, WIDE),
            pltpu.VMEM((n_in - 1, slots, js, share), NARROW),
        ] + [dma] * 6,
        compiler_params=pltpu.CompilerParams(collective_id=1, has_side_effects=True),
    )(s_home, cross, gram, yg)


def inverse_factor(gram, out_ref):
    count, size, _ = gram.shape
    tall = lax.broadcasted_iota(jnp.int32, (size, size), 0)
    wide = lax.broadcasted_iota(jnp.int32, (size, size), 1)
    eye = (tall == wide).astype(WIDE)
    lines = lax.broadcasted_iota(jnp.int32, (8, 1), 0)
    works = []
    for j in range(count):
        full = jnp.concatenate([gram[j], eye], axis=1)
        works.append([full[8 * b : 8 * b + 8] for b in range(size // 8)])
    scales = [[] for _ in range(count)]
    for k in range(size):
        b0, in_b = k // 8, k % 8
        for j in range(count):
            work = works[j]
            line = work[b0][in_b : in_b + 1]
            pivot = line[:, k : k + 1]
            scales[j].append(lax.rsqrt(pivot))
            line = line * (1.0 / pivot)
            for b in range(b0, size // 8):
                column = work[b][:, k : k + 1]
                if b == b0:
                    if in_b == 7:
                        continue
                    column = jnp.where(lines > in_b, column, 0.0)
                work[b] = work[b] - column * line
    for j in range(count):
        scale = jnp.concatenate(scales[j], axis=0)
        out_ref[j] = jnp.concatenate(works[j], axis=0)[:, size:] * scale


def local(sizes, near_flags, row_factor, col_factor, near_block, inner_left, inner_right, sketch_matrix):
    slots, own_j, rank, width = inner_left.shape
    js = own_j * rank
    cols = row_factor.shape[-1]
    mask = jnp.broadcast_to(near_flags[0].astype(WIDE)[:, None, None], (slots, 8, cols))
    s_home, cross, gram, yg = product(
        mask, row_factor[0], col_factor[0], near_block[0],
        inner_left.reshape(slots, js, width), inner_right.reshape(slots, js, width), sketch_matrix, sizes,
    )
    basis, coupling = factor(s_home, cross, gram, yg, sizes[2])
    return (basis[None], coupling[None])


def solution(mesh):
    sizes = (mesh.shape["row"], mesh.shape["col"], mesh.shape["inner"])
    in_specs = (
        P("row", "inner"),
        P("row", "inner", None, "col"),
        P("row", "inner", None, "col"),
        P("row", "inner", None, "col"),
        P("inner", "col", None, "row"),
        P("inner", "col", None, "row"),
        P("col", None, None),
    )
    out_specs = (P("row", "col", None, "inner"), P("row", "col", None, "inner"))
    return jax.shard_map(
        functools.partial(local, sizes), mesh=mesh, in_specs=in_specs, out_specs=out_specs, check_vma=False
    )
```

time: 259 us -> 171 us (0.66)
  the two profiles are of different devices: /device:TPU:0 before, /device:TPU:25 now
where the time goes in v1:
time: 171 us
  Pallas kernels  164 us (96%)
  local copies, waits for them, and re-layouts  5.31 us (3%)
    pallas_call x1, Pallas kernels, product(): pl.pallas_call(functools.partial(product_kernel, dims), out_shape=(jax.Sh...  132 us
    pallas_call x1, Pallas kernels, factor(): pl.pallas_call(functools.partial(factor_kernel, (n_in, slots, own_j, rank...  31.7 us
    unnamed x2, local copies, waits for them, and re-layouts  4.61 us

profile of v1, /device:TPU:25, one launch (start us, length us, event | category | flops | bytes accessed | tf_op | source)
XLA Modules:
  0.0 170.6 jit_solution(6573996318978407377)
XLA Ops:
  0.6 0.7 convert_bitcast_fusion
  1.3 0.7 broadcast_in_dim.12.mask_ref
  2.0 132.3 %shard_map.86 = (bf16[256,1024]{1,0:T(8,128)(2,1)}, f32[256,256]{1,0:T(8,128)}, f32[4,64,64]{2,1,0:T(8,128)}, bf16[3,256,2048]{2,1,0:T(8,128)(2,1)}) custom-call(f32[3,8,512]{2,1,0:T(8,128)} %broadcast_in_dim.12.mask_ref, bf16[3,64,512]{2,1,0:T(8,128)(2,1)} %bitcast.14, bf16[3,64,512]{2,1,0:T(8,128)(2,1)} %bitcast.15, bf16[3,2048,512]{2,1,0:T(8,128)(2,1)} %bitcast.9, ...), custom_call_target="tpu_custom_call" | custom-call | tf_op jit(solution)/shard_map/pallas_call | solution.py:452
  134.3 31.7 %shard_map.87 = (f32[4,64,1024]{2,1,0:T(8,128)}, f32[4,64,1024]{2,1,0:T(8,128)}) custom-call(bf16[256,1024]{1,0:T(8,128)(2,1)} %get-tuple-element.8.s_ref, f32[256,256]{1,0:T(8,128)} %get-tuple-element.9.cross_ref, f32[4,64,64]{2,1,0:T(8,128)} %get-tuple-element.10.gram_ref, bf16[3,256,2048]{2,1,0:T(8,128)(2,1)} %get-tuple-element.11.yg_ref), custom_call_target="tpu_custom_call" | custom-call | tf_op jit(solution)/shard_map/pallas_call | solution.py:561
  166.0 2.3 %copy.11 = f32[1,4,64,1024]{3,2,1,0:T(8,128)} copy(f32[1,4,64,1024]{3,2,1,0:T(8,128)} %bitcast.11) | data formatting | bytes 2097152
  168.3 2.3 %copy.12 = f32[1,4,64,1024]{3,2,1,0:T(8,128)} copy(f32[1,4,64,1024]{3,2,1,0:T(8,128)} %bitcast.10) | data formatting | bytes 2097152

commit v2 on v1

v2 whole, which is shorter than its diff:
```python
import functools
import math

import jax
import jax.numpy as jnp
from jax import lax
from jax.experimental import pallas as pl
from jax.experimental.pallas import tpu as pltpu
from jax.sharding import PartitionSpec as P

MESH = pl.DeviceIdType.MESH
HIGHEST = lax.Precision.HIGHEST
WIDE = jnp.float32
NARROW = jnp.bfloat16
NT = (((1,), (1,)), ((), ()))
TN = (((0,), (0,)), ((), ()))


def remote(src, dst, send, recv, device):
    return pltpu.make_async_remote_copy(
        src_ref=src, dst_ref=dst, send_sem=send, recv_sem=recv, device_id=device, device_id_type=MESH
    )


def meet(devices):
    barrier = pltpu.get_barrier_semaphore()
    for device in devices:
        pl.semaphore_signal(barrier, inc=1, device_id=device, device_id_type=MESH)
    pl.semaphore_wait(barrier, len(devices))


def split(value):
    high = value.astype(NARROW)
    return high, (value - high.astype(WIDE)).astype(NARROW)


def lanes(length):
    return -(-length // 128) * 128


def product_kernel(
    dims, flag_ref, u_ref, v_ref, d_ref, x_ref, y_ref, o_ref,
    basis_ref, coupling_ref,
    xg, vg, yg, yb, deff, pbuf, zt, zpart, zgot, zown, spart, ssend, sgot, msend, mgot, hsend, hrel, s_home,
    cross_sum, cross_got, inv,
    x_z_send, x_z_recv, x_f_send, x_f_recv, x_t_send, x_t_recv,
    v_send, v_recv, z_z_send, z_z_recv, z_f_send, z_f_recv, z_t_send, z_t_recv, zp_send, zp_recv,
    s_send, s_recv, m_send, m_recv, h_send, h_recv, r_send, r_recv, f_send, f_recv,
    y_f_send, y_f_recv, y_t_send, y_t_recv, y_y_send, y_y_recv, y_p_send, y_p_recv, c_send, c_recv, own,
):
    n_row, n_col, n_in, slots, own_j, rank, width, cols = dims
    js = own_j * rank
    half = js // 2
    kr = slots * rank
    total = n_row * width
    share = total // n_in
    group = n_col // n_in
    planes = n_row // 2
    zrows = js // n_row
    row, col, inner = lax.axis_index("row"), lax.axis_index("col"), lax.axis_index("inner")
    plane = lax.div(row, 2)
    parity = lax.rem(row, 2)
    twin = {"row": row + 1 - 2 * parity}
    far_planes = [lax.rem(plane + f, planes) for f in range(1, planes)]
    back_planes = [lax.rem(plane + planes - f, planes) for f in range(1, planes)]
    fars = [{"row": 2 * p + parity} for p in far_planes]
    up, down = {"col": lax.rem(col + 1, n_col)}, {"col": lax.rem(col + n_col - 1, n_col)}
    has = (col < n_col - 1, col > 0)
    row_peers = [lax.rem(row + d, n_row) for d in range(1, n_row)]
    in_peers = [lax.rem(inner + e, n_in) for e in range(1, n_in)]
    home = lax.div(col, group)
    helper = lax.rem(home + 1, n_in)
    helped = lax.rem(inner + n_in - 1, n_in)
    mine = pl.ds(pl.multiple_of(parity * half, half), half)

    fetches = [pltpu.make_async_copy(d_ref.at[k], deff.at[k], own.at[k]) for k in range(slots)]
    for fetch in fetches:
        fetch.start()

    meet(
        [{"row": r} for r in row_peers]
        + [{"col": lax.rem(col + d, n_col)} for d in range(1, n_col)]
        + [{"inner": p} for p in in_peers]
    )

    def at_rows(s):
        return pl.ds(pl.multiple_of(s * js, js), js)

    def x_at(s, k, p, q):
        return xg.at[k, at_rows(s), pl.ds(pl.multiple_of((2 * p + q) * width, width), width)]

    def v_at(s):
        return vg.at[:, :, pl.ds(pl.multiple_of(s * cols, cols), cols)]

    def z_at(s, p, q):
        return zt.at[s, pl.ds(pl.multiple_of((2 * p + q) * zrows, zrows), zrows)]

    def y_at(p, q):
        return yg.at[:, :, pl.ds(pl.multiple_of((2 * p + q) * width, width), width)]

    def x_line(s, k, way, src=None):
        place = x_at(s, k, plane, parity)
        return remote(
            place if src is None else src, place, x_z_send.at[way, s, k], x_z_recv.at[s, k], (up, down)[way]
        )

    def x_far(s, k, f, src=None):
        place = x_at(s, k, plane, parity)
        return remote(place if src is None else src, place, x_f_send.at[f, s, k], x_f_recv.at[f, s, k], fars[f])

    def x_twin(s, k, p, src=None):
        place = x_at(s, k, p, parity)
        return remote(place if src is None else src, place, x_t_send.at[p, s, k], x_t_recv.at[p, s, k], twin)

    def z_line(s, way, src=None):
        place = z_at(s, plane, parity)
        return remote(place if src is None else src, place, z_z_send.at[way, s], z_z_recv.at[s], (up, down)[way])

    def z_far(s, f, src=None):
        place = z_at(s, plane, parity)
        return remote(place if src is None else src, place, z_f_send.at[f, s], z_f_recv.at[f, s], fars[f])

    def z_twin(s, p, src=None):
        place = z_at(s, p, parity)
        return remote(place if src is None else src, place, z_t_send.at[p, s], z_t_recv.at[p, s], twin)

    def v_line(s, way, src=None):
        return remote(
            v_at(s) if src is None else src, v_at(s), v_send.at[way, s], v_recv.at[s], (up, down)[way]
        )

    def z_piece(d):
        rows = pl.ds(pl.multiple_of(row_peers[d] * zrows, zrows), zrows)
        return remote(zpart.at[rows], zgot.at[d], zp_send.at[d], zp_recv.at[d], {"row": row_peers[d]})

    def y_far(f):
        return remote(y_ref, y_at(plane, parity), y_f_send.at[f], y_f_recv.at[f], fars[f])

    def y_twin(p, src=None):
        place = y_at(p, parity)
        return remote(place if src is None else src, place, y_t_send.at[p], y_t_recv.at[p], twin)

    def y_inner(e):
        lane = pl.ds(pl.multiple_of(in_peers[e] * share, share), share)
        return remote(
            yg.at[:, mine, lane], yb.at[e, :, mine], y_y_send.at[e], y_y_recv.at[e], {"inner": in_peers[e]}
        )

    def y_pass(e):
        return remote(yb.at[e, :, mine], yb.at[e, :, mine], y_p_send.at[e], y_p_recv.at[e], twin)

    def share_plane(peer):
        return lax.div(peer * share, 2 * width)

    def s_peer(s, h, e):
        rows = pl.ds(h * half, half)
        return remote(
            ssend.at[s, rows], sgot.at[e, s, rows], s_send.at[e, s, h], s_recv.at[e, s, h], {"inner": in_peers[e]}
        )

    def m_home(s, h, source):
        return remote(msend.at[s, h], mgot.at[source, h], m_send.at[s, h], m_recv.at[source, h], {"col": s})

    def home_at(g, h):
        return s_home.at[pl.ds(h * half, half), pl.ds(pl.multiple_of(g * cols, cols), cols)]

    def h_home(s, g):
        return remote(hsend.at[s, pl.ds(0, half)], home_at(g, 0), h_send.at[s], h_recv.at[g], {"col": s})

    def h_relay(s, g):
        return remote(hsend.at[s, pl.ds(half, half)], hrel.at[g], r_send.at[s], r_recv.at[g], {"col": s})

    def h_pass(g, src=None):
        return remote(
            hrel.at[g] if src is None else src, home_at(g, 1), f_send.at[g], f_recv.at[g], {"inner": helped}
        )

    def c_inner(e):
        return remote(cross_sum, cross_got.at[e], c_send.at[e], c_recv.at[e], {"inner": in_peers[e]})

    def unit(b):
        both = jnp.minimum(col, n_col - 1 - col)
        near = lax.div(b + 1, 2)
        paired = jnp.where(lax.rem(b, 2) == 1, col - near, col + near)
        single = jnp.where(col < n_col - 1 - col, col + (b - both), col - (b - both))
        return jnp.where(b <= 2 * both, paired, single)

    def own_line(k):
        for way in range(2):

            @pl.when(has[way])
            def _(way=way):
                x_line(col, k, way, x_ref.at[k]).start()

    for way in range(2):

        @pl.when(has[way])
        def _(way=way):
            v_line(col, way, v_ref).start()

    own_line(0)
    for f in range(planes - 1):
        x_far(col, 0, f, x_ref.at[0]).start()
    y_twin(plane, y_ref).start()
    for k in range(slots):
        x_twin(col, k, plane, x_ref.at[k]).start()

    omega_at = pl.ds(pl.multiple_of(row * width, width), width)
    for j in range(own_j):
        inner_rows = jnp.concatenate([y_ref[k, j * rank : (j + 1) * rank] for k in range(slots)], axis=0)
        part = lax.dot_general(o_ref[j, :, omega_at], inner_rows, NT, preferred_element_type=WIDE)
        zpart[j * rank : (j + 1) * rank, 0:kr] = part
    for k in range(slots):
        xg[k, at_rows(col), pl.ds(pl.multiple_of(row * width, width), width)] = x_ref[k]
    vg[:, :, pl.ds(pl.multiple_of(col * cols, cols), cols)] = v_ref[...]
    yg[:, :, pl.ds(pl.multiple_of(row * width, width), width)] = y_ref[...]
    for d in range(n_row - 1):
        z_piece(d).start()
    for k in range(1, slots):
        for f in range(planes - 1):
            x_far(col, k, f, x_ref.at[k]).start()
    y_twin(plane).wait_recv()
    for e in range(n_in - 1):

        @pl.when(share_plane(in_peers[e]) == plane)
        def _(e=e):
            y_inner(e).start()

    def gather_z():
        total_z = zpart[pl.ds(pl.multiple_of(row * zrows, zrows), zrows), 0:kr]
        for d in range(n_row - 1):
            z_piece(d).wait_recv()
            total_z = total_z + zgot[d, :, 0:kr]
        quarter = total_z.astype(NARROW)
        zown[:, 0:kr] = quarter
        zt[col, pl.ds(pl.multiple_of(row * zrows, zrows), zrows), 0:kr] = quarter
        for way in range(2):

            @pl.when(has[way])
            def _(way=way):
                z_line(col, way, zown).start()

        for f in range(planes - 1):
            z_far(col, f, zown).start()
        z_twin(col, plane, zown).start()

    def along(t, act):
        for way in range(2):
            s = col - t if way == 0 else col + t

            @pl.when(s >= 0 if way == 0 else s < n_col)
            def _(s=s, way=way):
                act(s, way)

    def pass_v(s, way):
        v_line(s, way).wait_recv()

        @pl.when(has[way])
        def _():
            v_line(s, way).start()

    def pass_z(s, way):
        z_line(s, way).wait_recv()

        @pl.when(has[way])
        def _():
            z_line(s, way).start()

        z_twin(s, plane).start()

    def pump(b, k):
        def pass_x(s, way):
            x_line(s, k, way).wait_recv()

            @pl.when(has[way])
            def _():
                x_line(s, k, way).start()

            x_twin(s, k, plane).start()

        along(b + 1, pass_x)

        @pl.when(b + 1 < n_col)
        def _():
            ahead = unit(b + 1)
            for f in range(planes - 1):
                x_far(ahead, k, f).start()

        here = unit(b)

        @pl.when(jnp.logical_and(k == 0, b > 0))
        def _():
            along(b, pass_z)
            for f in range(planes - 1):
                z_far(here, f).start()

        for f in range(planes - 1):
            x_far(here, k, f).wait_recv()
            x_twin(here, k, back_planes[f]).start()

        @pl.when(k == slots - 1)
        def _():
            for f in range(planes - 1):
                z_far(here, f).wait_recv()
                z_twin(here, back_planes[f]).start()

    step_rows = min(512, total)

    def effective(k):
        pltpu.make_async_copy(d_ref.at[k], deff.at[k], own.at[k]).wait()
        near = jnp.full((1, cols), flag_ref[0, k], jnp.int32) > 0

        def some(i, carry):
            at = pl.ds(pl.multiple_of(i * step_rows, step_rows), step_rows)
            low = lax.dot_general(vg[k, :, at], u_ref[k], TN, preferred_element_type=WIDE)
            dense = deff[k, at, :].astype(WIDE)
            deff[k, at, :] = jnp.where(near, dense, low).astype(NARROW)
            return carry

        lax.fori_loop(0, total // step_rows, some, 0)

    def piece(b, k):
        @pl.when(b == 0)
        def _():
            effective(k)

        s = unit(b)
        for p in range(planes):
            x_twin(s, k, p).wait_recv()
        out = jnp.dot(xg[k, at_rows(s), :], deff[k], preferred_element_type=WIDE).astype(NARROW)
        for j in range(own_j):
            pbuf[s, j, pl.ds(pl.multiple_of(k * rank, rank), rank), :] = out[j * rank : (j + 1) * rank]

    def sample(b):
        s = unit(b)
        for p in range(planes):
            z_twin(s, p).wait_recv()
        for h in range(2):
            for j in range(h * own_j // 2, (h + 1) * own_j // 2):
                rows = slice(j * rank, (j + 1) * rank)
                part = jnp.dot(zt[s, rows, 0:kr], pbuf[s, j], preferred_element_type=WIDE)
                spart[s, rows, :] = part
                ssend[s, rows, :] = part.astype(NARROW)
            for e in range(n_in - 1):
                s_peer(s, h, e).start()

    def finish(b):
        s = unit(b)
        away = s != col
        lane = lax.rem(col, group)
        for h in range(2):
            for e in range(n_in - 1):
                s_peer(s, h, e).wait_recv()
            lows = []
            for i in range(own_j // 2):
                j = h * (own_j // 2) + i
                rows = slice(j * rank, (j + 1) * rank)
                whole = spart[s, rows, :]
                for e in range(n_in - 1):
                    whole = whole + sgot[e, s, rows, :].astype(WIDE)
                high, low = split(whole)
                hsend[s, rows, :] = high
                left = jnp.concatenate([high, low], axis=0)
                right = jnp.concatenate([pbuf[s, j], left], axis=0)
                both = lax.dot_general(left, right, NT, preferred_element_type=WIDE)
                top, under = both[:rank], both[rank:]
                cross = top[:, :kr] + under[:, :kr]
                gram = top[:, kr : kr + rank] + top[:, kr + rank :] + under[:, kr : kr + rank]
                gram_high, gram_low = split(gram)
                at = slice(i * rank, (i + 1) * rank)
                msend[s, h, at, 0:kr] = cross.astype(NARROW)
                msend[s, h, at, kr : kr + rank] = gram_high
                lows.append(gram_low)
            pair = jnp.concatenate(lows, axis=1)
            folds = (kr + rank) // pair.shape[1]
            deep = rank // folds
            msend[s, h, half : half + deep] = jnp.concatenate(
                [pair[i * deep : (i + 1) * deep] for i in range(folds)], axis=1
            )

            @pl.when(away)
            def _(h=h):
                m_home(s, h, col).start()

            if h == 0:

                @pl.when(jnp.logical_and(away, home == inner))
                def _():
                    h_home(s, lane).start()

            else:

                @pl.when(jnp.logical_and(away, helper == inner))
                def _():
                    h_relay(s, lane).start()

        @pl.when(jnp.logical_not(away))
        def _():
            mgot[col] = msend[s]

            @pl.when(home == inner)
            def _():
                s_home[0:half, pl.ds(pl.multiple_of(lane * cols, cols), cols)] = hsend[s, 0:half]

    count = n_col * slots
    ready = n_col - 2

    def done(q):
        return jnp.maximum(jnp.minimum(q, 2 * (q - ready + 1)), 0)

    def work(i, carry):
        b, k = lax.div(i, slots), lax.rem(i, slots)
        piece(b, k)

        @pl.when(k == slots - 1)
        def _():
            sample(b)

        @pl.when(jnp.logical_and(k == min(1, slots - 1), b > 0))
        def _():
            finish(b - 1)

        return carry

    def step(q, carry):
        @pl.when(q < n_col - 1)
        def _():
            along(q + 1, pass_v)

        @pl.when(q + 1 < slots)
        def _():
            own_line(q + 1)

        @pl.when(q < count)
        def _():
            pump(lax.div(q, slots), lax.rem(q, slots))

        @pl.when(q == 0)
        def _():
            gather_z()

        @pl.when(q == (n_col - 1) * slots)
        def _():
            for f in range(planes - 1):
                y_far(f).start()

        lax.fori_loop(done(q - 1), done(q), work, 0)
        return carry

    lax.fori_loop(0, count + 1, step, 0)
    finish(n_col - 1)

    for f in range(planes - 1):
        y_far(f).wait_recv()
        y_twin(back_planes[f]).start()
    for g in range(group):
        source = helped * group + g

        @pl.when(source != col)
        def _(g=g, source=source):
            h_relay(source, g).wait_recv()
            h_pass(g).start()

        @pl.when(source == col)
        def _(g=g):
            h_pass(g, hsend.at[col, pl.ds(half, half)]).start()

    for f in range(planes - 1):
        y_twin(back_planes[f]).wait_recv()
    for e in range(n_in - 1):

        @pl.when(share_plane(in_peers[e]) != plane)
        def _(e=e):
            y_inner(e).start()

    for d in range(1, n_col):
        source = lax.rem(col + d, n_col)
        for h in range(2):
            m_home(source, h, source).wait_recv()
    grams = []
    for h in range(2):
        crosses = mgot[0, h, 0:half, 0:kr].astype(WIDE)
        high = mgot[0, h, 0:half, kr : kr + rank].astype(WIDE)
        deep = msend.shape[2] - half
        under = mgot[0, h, half : half + deep].astype(WIDE)
        for c in range(1, n_col):
            crosses = crosses + mgot[c, h, 0:half, 0:kr].astype(WIDE)
            high = high + mgot[c, h, 0:half, kr : kr + rank].astype(WIDE)
            under = under + mgot[c, h, half : half + deep].astype(WIDE)
        cross_sum[h * half : (h + 1) * half, 0:kr] = crosses
        wide = half
        pair = jnp.concatenate([under[:, i * wide : (i + 1) * wide] for i in range(under.shape[1] // wide)], axis=0)
        for i in range(own_j // 2):
            grams.append(high[i * rank : (i + 1) * rank] + pair[:, i * rank : (i + 1) * rank])
    for e in range(n_in - 1):
        c_inner(e).start()
    inverse_factor(grams, inv)

    for g in range(group):
        source = inner * group + g

        @pl.when(source != col)
        def _(g=g, source=source):
            h_home(source, g).wait_recv()

        h_pass(g).wait_recv()
    for e in range(n_in - 1):
        y_inner(e).wait_recv()
        y_pass(e).start()
    for j in range(own_j):
        rows = slice(j * rank, (j + 1) * rank)
        both = jnp.concatenate(split(inv[j]), axis=0)
        out = jnp.dot(both, s_home[rows, :], preferred_element_type=WIDE)
        basis_ref[j] = out[:rank] + out[rank:]
    for e in range(n_in - 1):
        c_inner(e).wait_recv()
    left = []
    for j in range(own_j):
        rows = slice(j * rank, (j + 1) * rank)
        crossed = jnp.concatenate(
            [cross_sum[rows, 0:kr]] + [cross_got[e, rows, 0:kr] for e in range(n_in - 1)], axis=1
        )
        projected = jnp.dot(inv[j], crossed, precision=HIGHEST, preferred_element_type=WIDE)
        left.append(jnp.concatenate(split(projected), axis=0))
    for e in range(n_in - 1):
        y_pass(e).wait_recv()
    lane_own = pl.ds(pl.multiple_of(inner * share, share), share)
    for j in range(own_j):
        rows = slice(j * rank, (j + 1) * rank)
        right = [yg[k, rows, lane_own] for k in range(slots)]
        right += [yb[e, k, rows, :] for e in range(n_in - 1) for k in range(slots)]
        out = jnp.dot(left[j], jnp.concatenate(right, axis=0), preferred_element_type=WIDE)
        coupling_ref[j] = out[:rank] + out[rank:]

    for p in range(planes):
        y_twin(p).wait_send()
    for f in range(planes - 1):
        y_far(f).wait_send()
    for d in range(n_row - 1):
        z_piece(d).wait_send()
    for e in range(n_in - 1):
        y_inner(e).wait_send()
        y_pass(e).wait_send()
        c_inner(e).wait_send()
    for g in range(group):
        h_pass(g).wait_send()

    def drain(s, carry):
        for way in range(2):

            @pl.when(jnp.logical_and(has[way], s <= col if way == 0 else s >= col))
            def _(way=way):
                v_line(s, way).wait_send()
                z_line(s, way).wait_send()
                for k in range(slots):
                    x_line(s, k, way).wait_send()

        for f in range(planes - 1):
            z_far(s, f).wait_send()
            for k in range(slots):
                x_far(s, k, f).wait_send()
        for p in range(planes):
            z_twin(s, p).wait_send()
            for k in range(slots):
                x_twin(s, k, p).wait_send()
        for e in range(n_in - 1):
            for h in range(2):
                s_peer(s, h, e).wait_send()

        @pl.when(s != col)
        def _():
            for h in range(2):
                m_home(s, h, col).wait_send()

            @pl.when(home == inner)
            def _():
                h_home(s, 0).wait_send()

            @pl.when(helper == inner)
            def _():
                h_relay(s, 0).wait_send()

        return carry

    lax.fori_loop(0, n_col, drain, 0)


def product(flags, u, v, d, x, y, omega, sizes):
    n_row, n_col, n_in = sizes
    slots, js, width = x.shape
    own_j, rank, total = omega.shape
    cols = u.shape[-1]
    planes = n_row // 2
    kr = slots * rank
    group = n_col // n_in
    share = total // n_in
    half = js // 2
    packed = half + rank * (own_j // 2) * rank // (kr + rank)
    vmem = pl.BlockSpec(memory_space=pltpu.VMEM)
    dma = pltpu.SemaphoreType.DMA
    dims = (n_row, n_col, n_in, slots, own_j, rank, width, cols)
    out = jax.ShapeDtypeStruct((own_j, rank, share), WIDE)
    return pl.pallas_call(
        functools.partial(product_kernel, dims),
        out_shape=(out, out),
        in_specs=[
            pl.BlockSpec(memory_space=pltpu.SMEM), vmem, vmem, pl.BlockSpec(memory_space=pltpu.HBM), vmem, vmem, vmem
        ],
        out_specs=[vmem] * 2,
        scratch_shapes=[
            pltpu.VMEM((slots, n_col * js, total), NARROW),
            pltpu.VMEM((slots, rank, total), NARROW),
            pltpu.VMEM((slots, js, total), NARROW),
            pltpu.VMEM((n_in - 1, slots, js, share), NARROW),
            pltpu.VMEM((slots, total, cols), NARROW),
            pltpu.VMEM((n_col, own_j, kr, cols), NARROW),
            pltpu.VMEM((n_col, js, lanes(kr)), NARROW),
            pltpu.VMEM((js, lanes(kr)), WIDE),
            pltpu.VMEM((n_row - 1, js // n_row, lanes(kr)), WIDE),
            pltpu.VMEM((js // n_row, lanes(kr)), NARROW),
            pltpu.VMEM((n_col, js, cols), WIDE),
            pltpu.VMEM((n_col, js, cols), NARROW),
            pltpu.VMEM((n_in - 1, n_col, js, cols), NARROW),
            pltpu.VMEM((n_col, 2, packed, kr + rank), NARROW),
            pltpu.VMEM((n_col, 2, packed, kr + rank), NARROW),
            pltpu.VMEM((n_col, js, cols), NARROW),
            pltpu.VMEM((group, half, cols), NARROW),
            pltpu.VMEM((js, share), NARROW),
            pltpu.VMEM((js, lanes(kr)), WIDE),
            pltpu.VMEM((n_in - 1, js, lanes(kr)), WIDE),
            pltpu.VMEM((own_j, rank, rank), WIDE),
            dma((2, n_col, slots)), dma((n_col, slots)),
            dma((planes - 1, n_col, slots)), dma((planes - 1, n_col, slots)),
            dma((planes, n_col, slots)), dma((planes, n_col, slots)),
            dma((2, n_col)), dma((n_col,)),
            dma((2, n_col)), dma((n_col,)),
            dma((planes - 1, n_col)), dma((planes - 1, n_col)),
            dma((planes, n_col)), dma((planes, n_col)),
            dma((n_row - 1,)), dma((n_row - 1,)),
            dma((n_in - 1, n_col, 2)), dma((n_in - 1, n_col, 2)),
            dma((n_col, 2)), dma((n_col, 2)),
            dma((n_col,)), dma((group,)),
            dma((n_col,)), dma((group,)),
            dma((group,)), dma((group,)),
            dma((planes - 1,)), dma((planes - 1,)),
            dma((planes,)), dma((planes,)),
            dma((n_in - 1,)), dma((n_in - 1,)),
            dma((n_in - 1,)), dma((n_in - 1,)),
            dma((n_in - 1,)), dma((n_in - 1,)),
            dma((slots,)),
        ],
        compiler_params=pltpu.CompilerParams(
            collective_id=0, has_side_effects=True, vmem_limit_bytes=60 * 1024 * 1024
        ),
    )(flags, u, v, d, x, y, omega)


def inverse_factor(gram, out_ref):
    count, size = len(gram), gram[0].shape[0]
    tall = lax.broadcasted_iota(jnp.int32, (size, size), 0)
    wide = lax.broadcasted_iota(jnp.int32, (size, size), 1)
    eye = (tall == wide).astype(WIDE)
    lines = lax.broadcasted_iota(jnp.int32, (8, 1), 0)
    works = []
    for j in range(count):
        full = jnp.concatenate([gram[j], eye], axis=1)
        works.append([full[8 * b : 8 * b + 8] for b in range(size // 8)])
    scales = [[] for _ in range(count)]
    for k in range(size):
        b0, in_b = k // 8, k % 8
        for j in range(count):
            work = works[j]
            line = work[b0][in_b : in_b + 1]
            pivot = line[:, k : k + 1]
            scales[j].append(lax.rsqrt(pivot))
            line = line * (1.0 / pivot)
            for b in range(b0, size // 8):
                column = work[b][:, k : k + 1]
                if b == b0:
                    if in_b == 7:
                        continue
                    column = jnp.where(lines > in_b, column, 0.0)
                work[b] = work[b] - column * line
    for j in range(count):
        scale = jnp.concatenate(scales[j], axis=0)
        out_ref[j] = jnp.concatenate(works[j], axis=0)[:, size:] * scale


def local(sizes, near_flags, row_factor, col_factor, near_block, inner_left, inner_right, sketch_matrix):
    slots, own_j, rank, width = inner_left.shape
    js = own_j * rank
    basis, coupling = product(
        near_flags, row_factor[0], col_factor[0], near_block[0],
        inner_left.reshape(slots, js, width), inner_right.reshape(slots, js, width), sketch_matrix, sizes,
    )
    return (basis[None] * math.sqrt(width * sizes[0]), coupling[None])


def solution(mesh):
    sizes = (mesh.shape["row"], mesh.shape["col"], mesh.shape["inner"])
    in_specs = (
        P("row", "inner"),
        P("row", "inner", None, "col"),
        P("row", "inner", None, "col"),
        P("row", "inner", None, "col"),
        P("inner", "col", None, "row"),
        P("inner", "col", None, "row"),
        P("col", None, None),
    )
    out_specs = (P("row", "col", None, "inner"), P("row", "col", None, "inner"))
    return jax.shard_map(
        functools.partial(local, sizes), mesh=mesh, in_specs=in_specs, out_specs=out_specs, check_vma=False
    )
```

time: 171 us -> 146 us (0.85)
  the two profiles are of different devices: /device:TPU:25 before, /device:TPU:0 now
where the time goes in v2:
time: 146 us; the launch traced here: 145 us
  Pallas kernels  140 us (96%)
  other arithmetic  2.35 us (2%)
  local copies, waits for them, and re-layouts  2.31 us (2%)
    pallas_call x1, Pallas kernels, product(): pl.pallas_call(functools.partial(product_kernel, dims), out_shape=(out, o...  140 us

profile of v2, /device:TPU:0, one launch (start us, length us, event | category | flops | bytes accessed | tf_op | source)
XLA Modules:
  0.0 145.3 jit_solution(15473267268671321381)
XLA Ops:
  0.6 140.0 %shard_map.86 = (f32[4,64,1024]{2,1,0:T(8,128)}, f32[4,64,1024]{2,1,0:T(8,128)}) custom-call(s32[1,3]{1,0:T(1,128)} %flag_ref.1, bf16[3,64,512]{2,1,0:T(8,128)(2,1)} %bitcast.12, bf16[3,64,512]{2,1,0:T(8,128)(2,1)} %bitcast.13, bf16[3,2048,512]{2,1,0:T(8,128)(2,1)} %bitcast.8, bf16[3,256,512]{2,1,0:T(8,128)(2,1)} %bitcast.10, bf16[3,256,512]{2,1,0:T(8,128)(2,1)} %bitcast.11, ...), custom_call_target="tpu_custom_call" | custom-call | tf_op jit(solution)/shard_map/pallas_call | solution.py:603
  140.6 2.3 %multiply_bitcast_fusion = f32[1,4,64,1024]{3,2,1,0:T(8,128)} fusion(f32[4,64,1024]{2,1,0:T(8,128)} %get-tuple-element.4), kind=kLoop, calls=%fused_computation | loop fusion | flops 262144 | bytes 2097152 | tf_op jit(solution)/shard_map/mul | solution.py:696
  143.0 2.3 %copy.10 = f32[1,4,64,1024]{3,2,1,0:T(8,128)} copy(f32[1,4,64,1024]{3,2,1,0:T(8,128)} %bitcast.9) | data formatting | bytes 2097152

commit v3 on v2

--- a/solution.py
+++ b/solution.py
@@ -39,14 +39,15 @@
 
 
 def product_kernel(
-    dims, flag_ref, u_ref, v_ref, d_ref, x_ref, y_ref, o_ref,
+    dims, flag_ref, u_hbm, v_hbm, d_ref, x_hbm, y_hbm, o_hbm,
     basis_ref, coupling_ref,
+    u_ref, o_ref,
     xg, vg, yg, yb, deff, pbuf, zt, zpart, zgot, zown, spart, ssend, sgot, msend, mgot, hsend, hrel, s_home,
-    cross_sum, cross_got, inv,
-    x_z_send, x_z_recv, x_f_send, x_f_recv, x_t_send, x_t_recv,
+    cross_sum, cross_pass, cross_got, inv,
+    x_z_send, x_z_recv, x_f_send, x_f_recv, x_t_send, x_t_recv, x_s_send, x_s_recv,
     v_send, v_recv, z_z_send, z_z_recv, z_f_send, z_f_recv, z_t_send, z_t_recv, zp_send, zp_recv,
     s_send, s_recv, m_send, m_recv, h_send, h_recv, r_send, r_recv, f_send, f_recv,
-    y_f_send, y_f_recv, y_t_send, y_t_recv, y_y_send, y_y_recv, y_p_send, y_p_recv, c_send, c_recv, own,
+    y_f_send, y_f_recv, y_t_send, y_t_recv, y_y_send, y_y_recv, y_p_send, y_p_recv, c_send, c_recv, own, x_own, y_own, v_own,
 ):
     n_row, n_col, n_in, slots, own_j, rank, width, cols = dims
     js = own_j * rank
@@ -66,6 +67,8 @@
     fars = [{"row": 2 * p + parity} for p in far_planes]
     up, down = {"col": lax.rem(col + 1, n_col)}, {"col": lax.rem(col + n_col - 1, n_col)}
     has = (col < n_col - 1, col > 0)
+    middle = jnp.logical_and(has[0], has[1])
+    beside = (col + 1 < n_col - 1, col - 1 > 0)
     row_peers = [lax.rem(row + d, n_row) for d in range(1, n_row)]
     in_peers = [lax.rem(inner + e, n_in) for e in range(1, n_in)]
     home = lax.div(col, group)
@@ -73,16 +76,6 @@
     helped = lax.rem(inner + n_in - 1, n_in)
     mine = pl.ds(pl.multiple_of(parity * half, half), half)
 
-    fetches = [pltpu.make_async_copy(d_ref.at[k], deff.at[k], own.at[k]) for k in range(slots)]
-    for fetch in fetches:
-        fetch.start()
-
-    meet(
-        [{"row": r} for r in row_peers]
-        + [{"col": lax.rem(col + d, n_col)} for d in range(1, n_col)]
-        + [{"inner": p} for p in in_peers]
-    )
-
     def at_rows(s):
         return pl.ds(pl.multiple_of(s * js, js), js)
 
@@ -95,8 +88,8 @@
     def z_at(s, p, q):
         return zt.at[s, pl.ds(pl.multiple_of((2 * p + q) * zrows, zrows), zrows)]
 
-    def y_at(p, q):
-        return yg.at[:, :, pl.ds(pl.multiple_of((2 * p + q) * width, width), width)]
+    def y_at(k, p, q):
+        return yg.at[k, :, pl.ds(pl.multiple_of((2 * p + q) * width, width), width)]
 
     def x_line(s, k, way, src=None):
         place = x_at(s, k, plane, parity)
@@ -133,29 +126,33 @@
         rows = pl.ds(pl.multiple_of(row_peers[d] * zrows, zrows), zrows)
         return remote(zpart.at[rows], zgot.at[d], zp_send.at[d], zp_recv.at[d], {"row": row_peers[d]})
 
-    def y_far(f):
-        return remote(y_ref, y_at(plane, parity), y_f_send.at[f], y_f_recv.at[f], fars[f])
-
-    def y_twin(p, src=None):
-        place = y_at(p, parity)
-        return remote(place if src is None else src, place, y_t_send.at[p], y_t_recv.at[p], twin)
-
-    def y_inner(e):
+    def x_side(k, f, way):
+        place = x_at(col, k, back_planes[f], parity)
+        return remote(place, place, x_s_send.at[f, way, k], x_s_recv.at[f, way, k], (up, down)[way])
+
+    def y_far(f, k):
+        return remote(y_at(k, plane, parity), y_at(k, plane, parity), y_f_send.at[f, k], y_f_recv.at[f, k], fars[f])
+
+    def y_twin(p, k, src=None):
+        place = y_at(k, p, parity)
+        return remote(place if src is None else src, place, y_t_send.at[p, k], y_t_recv.at[p, k], twin)
+
+    def y_inner(e, k):
         lane = pl.ds(pl.multiple_of(in_peers[e] * share, share), share)
         return remote(
-            yg.at[:, mine, lane], yb.at[e, :, mine], y_y_send.at[e], y_y_recv.at[e], {"inner": in_peers[e]}
+            yg.at[k, mine, lane], yb.at[e, k, mine], y_y_send.at[e, k], y_y_recv.at[e, k], {"inner": in_peers[e]}
         )
 
-    def y_pass(e):
-        return remote(yb.at[e, :, mine], yb.at[e, :, mine], y_p_send.at[e], y_p_recv.at[e], twin)
+    def y_pass(e, k):
+        return remote(yb.at[e, k, mine], yb.at[e, k, mine], y_p_send.at[e, k], y_p_recv.at[e, k], twin)
 
     def share_plane(peer):
         return lax.div(peer * share, 2 * width)
 
-    def s_peer(s, h, e):
-        rows = pl.ds(h * half, half)
+    def s_peer(s, j, e):
+        rows = pl.ds(j * rank, rank)
         return remote(
-            ssend.at[s, rows], sgot.at[e, s, rows], s_send.at[e, s, h], s_recv.at[e, s, h], {"inner": in_peers[e]}
+            ssend.at[s, rows], sgot.at[e, s, rows], s_send.at[e, s, j], s_recv.at[e, s, j], {"inner": in_peers[e]}
         )
 
     def m_home(s, h, source):
@@ -176,7 +173,7 @@
         )
 
     def c_inner(e):
-        return remote(cross_sum, cross_got.at[e], c_send.at[e], c_recv.at[e], {"inner": in_peers[e]})
+        return remote(cross_pass, cross_got.at[e], c_send.at[e], c_recv.at[e], {"inner": in_peers[e]})
 
     def unit(b):
         both = jnp.minimum(col, n_col - 1 - col)
@@ -190,41 +187,65 @@
 
             @pl.when(has[way])
             def _(way=way):
-                x_line(col, k, way, x_ref.at[k]).start()
+                x_line(col, k, way).start()
+
+    here_rows = pl.ds(pl.multiple_of(row * width, width), width)
+    x_in = [
+        pltpu.make_async_copy(x_hbm.at[k], x_at(col, k, plane, parity), x_own.at[k]) for k in range(slots)
+    ]
+    v_in = pltpu.make_async_copy(v_hbm, v_at(col), v_own.at[0])
+    y_in = [pltpu.make_async_copy(y_hbm.at[k], y_at(k, plane, parity), y_own.at[k]) for k in range(slots)]
+    o_in = pltpu.make_async_copy(o_hbm.at[:, :, here_rows], o_ref, v_own.at[1])
+    u_in = pltpu.make_async_copy(u_hbm, u_ref, v_own.at[2])
+    for fetch in [v_in] + x_in + y_in + [o_in, u_in]:
+        fetch.start()
+    for k in range(slots):
+        pltpu.make_async_copy(d_ref.at[k], deff.at[k], own.at[k]).start()
+
+    for fetch in [v_in] + x_in:
+        fetch.wait()
+    for fetch in y_in + [o_in, u_in]:
+        fetch.wait()
+    for j in range(own_j):
+        inner_rows = jnp.concatenate(
+            [yg[k, j * rank : (j + 1) * rank, here_rows] for k in range(slots)], axis=0
+        )
+        part = lax.dot_general(o_ref[j], inner_rows, NT, preferred_element_type=WIDE)
+        zpart[j * rank : (j + 1) * rank, 0:kr] = part
+    meet(
+        [{"row": r} for r in row_peers]
+        + [{"col": lax.rem(col + d, n_col)} for d in range(1, n_col)]
+        + [{"inner": p} for p in in_peers]
+    )
 
     for way in range(2):
 
         @pl.when(has[way])
         def _(way=way):
-            v_line(col, way, v_ref).start()
-
-    own_line(0)
+            v_line(col, way).start()
+
+    for k in range(min(2, slots)):
+        own_line(k)
     for f in range(planes - 1):
-        x_far(col, 0, f, x_ref.at[0]).start()
-    y_twin(plane, y_ref).start()
+        x_far(col, 0, f).start()
     for k in range(slots):
-        x_twin(col, k, plane, x_ref.at[k]).start()
-
-    omega_at = pl.ds(pl.multiple_of(row * width, width), width)
-    for j in range(own_j):
-        inner_rows = jnp.concatenate([y_ref[k, j * rank : (j + 1) * rank] for k in range(slots)], axis=0)
-        part = lax.dot_general(o_ref[j, :, omega_at], inner_rows, NT, preferred_element_type=WIDE)
-        zpart[j * rank : (j + 1) * rank, 0:kr] = part
+        y_twin(plane, k).start()
     for k in range(slots):
-        xg[k, at_rows(col), pl.ds(pl.multiple_of(row * width, width), width)] = x_ref[k]
-    vg[:, :, pl.ds(pl.multiple_of(col * cols, cols), cols)] = v_ref[...]
-    yg[:, :, pl.ds(pl.multiple_of(row * width, width), width)] = y_ref[...]
+        x_twin(col, k, plane).start()
+
     for d in range(n_row - 1):
         z_piece(d).start()
     for k in range(1, slots):
         for f in range(planes - 1):
-            x_far(col, k, f, x_ref.at[k]).start()
-    y_twin(plane).wait_recv()
+            x_far(col, k, f).start()
+    for k in range(slots):
+        y_twin(plane, k).wait_recv()
     for e in range(n_in - 1):
 
         @pl.when(share_plane(in_peers[e]) == plane)
         def _(e=e):
-            y_inner(e).start()
+            for k in range(slots):
+                y_inner(e, k).start()
 
     def gather_z():
         total_z = zpart[pl.ds(pl.multiple_of(row * zrows, zrows), zrows), 0:kr]
@@ -278,14 +299,12 @@
 
             x_twin(s, k, plane).start()
 
+            @pl.when(jnp.logical_not(jnp.logical_and(middle, b == 0)))
+            def _():
+                for f in range(planes - 1):
+                    x_far(s, k, f).start()
+
         along(b + 1, pass_x)
-
-        @pl.when(b + 1 < n_col)
-        def _():
-            ahead = unit(b + 1)
-            for f in range(planes - 1):
-                x_far(ahead, k, f).start()
-
         here = unit(b)
 
         @pl.when(jnp.logical_and(k == 0, b > 0))
@@ -294,8 +313,28 @@
             for f in range(planes - 1):
                 z_far(here, f).start()
 
+        below = jnp.logical_and(middle, here == col - 1)
+        above = jnp.logical_and(middle, here == col + 1)
         for f in range(planes - 1):
-            x_far(here, k, f).wait_recv()
+
+            @pl.when(below)
+            def _(f=f):
+                x_side(k, f, 0).wait_recv()
+
+            @pl.when(above)
+            def _(f=f):
+                x_side(k, f, 1).wait_recv()
+
+            @pl.when(jnp.logical_not(jnp.logical_or(below, above)))
+            def _(f=f):
+                x_far(here, k, f).wait_recv()
+
+            for way in range(2):
+
+                @pl.when(jnp.logical_and(b == 0, beside[way]))
+                def _(f=f, way=way):
+                    x_side(k, f, way).start()
+
             x_twin(here, k, back_planes[f]).start()
 
         @pl.when(k == slots - 1)
@@ -335,26 +374,25 @@
         s = unit(b)
         for p in range(planes):
             z_twin(s, p).wait_recv()
-        for h in range(2):
-            for j in range(h * own_j // 2, (h + 1) * own_j // 2):
-                rows = slice(j * rank, (j + 1) * rank)
-                part = jnp.dot(zt[s, rows, 0:kr], pbuf[s, j], preferred_element_type=WIDE)
-                spart[s, rows, :] = part
-                ssend[s, rows, :] = part.astype(NARROW)
+        for j in range(own_j):
+            rows = slice(j * rank, (j + 1) * rank)
+            part = jnp.dot(zt[s, rows, 0:kr], pbuf[s, j], preferred_element_type=WIDE)
+            spart[s, rows, :] = part
+            ssend[s, rows, :] = part.astype(NARROW)
             for e in range(n_in - 1):
-                s_peer(s, h, e).start()
+                s_peer(s, j, e).start()
 
     def finish(b):
         s = unit(b)
         away = s != col
         lane = lax.rem(col, group)
         for h in range(2):
-            for e in range(n_in - 1):
-                s_peer(s, h, e).wait_recv()
             lows = []
             for i in range(own_j // 2):
                 j = h * (own_j // 2) + i
                 rows = slice(j * rank, (j + 1) * rank)
+                for e in range(n_in - 1):
+                    s_peer(s, j, e).wait_recv()
                 whole = spart[s, rows, :]
                 for e in range(n_in - 1):
                     whole = whole + sgot[e, s, rows, :].astype(WIDE)
@@ -422,27 +460,48 @@
 
         return carry
 
+    def start_y():
+        for f in range(planes - 1):
+            for k in range(slots):
+                y_far(f, k).start()
+
+    def pass_y():
+        for k in range(slots):
+            for f in range(planes - 1):
+                y_far(f, k).wait_recv()
+                y_twin(back_planes[f], k).start()
+            for f in range(planes - 1):
+                y_twin(back_planes[f], k).wait_recv()
+            for e in range(n_in - 1):
+
+                @pl.when(share_plane(in_peers[e]) != plane)
+                def _(e=e, k=k):
+                    y_inner(e, k).start()
+
     def step(q, carry):
+        @pl.when(q < count)
+        def _():
+            pump(lax.div(q, slots), lax.rem(q, slots))
+
         @pl.when(q < n_col - 1)
         def _():
             along(q + 1, pass_v)
 
-        @pl.when(q + 1 < slots)
-        def _():
-            own_line(q + 1)
-
-        @pl.when(q < count)
-        def _():
-            pump(lax.div(q, slots), lax.rem(q, slots))
+        @pl.when(q + 2 < slots)
+        def _():
+            own_line(q + 2)
 
         @pl.when(q == 0)
         def _():
             gather_z()
 
-        @pl.when(q == (n_col - 1) * slots)
-        def _():
-            for f in range(planes - 1):
-                y_far(f).start()
+        @pl.when(q == jnp.where(middle, 0, (n_col - 1) * slots))
+        def _():
+            start_y()
+
+        @pl.when(jnp.logical_and(middle, q == 2 * slots))
+        def _():
+            pass_y()
 
         lax.fori_loop(done(q - 1), done(q), work, 0)
         return carry
@@ -450,9 +509,10 @@
     lax.fori_loop(0, count + 1, step, 0)
     finish(n_col - 1)
 
-    for f in range(planes - 1):
-        y_far(f).wait_recv()
-        y_twin(back_planes[f]).start()
+    @pl.when(jnp.logical_not(middle))
+    def _():
+        pass_y()
+
     for g in range(group):
         source = helped * group + g
 
@@ -464,14 +524,6 @@
         @pl.when(source == col)
         def _(g=g):
             h_pass(g, hsend.at[col, pl.ds(half, half)]).start()
-
-    for f in range(planes - 1):
-        y_twin(back_planes[f]).wait_recv()
-    for e in range(n_in - 1):
-
-        @pl.when(share_plane(in_peers[e]) != plane)
-        def _(e=e):
-            y_inner(e).start()
 
     for d in range(1, n_col):
         source = lax.rem(col + d, n_col)
@@ -488,6 +540,7 @@
             high = high + mgot[c, h, 0:half, kr : kr + rank].astype(WIDE)
             under = under + mgot[c, h, half : half + deep].astype(WIDE)
         cross_sum[h * half : (h + 1) * half, 0:kr] = crosses
+        cross_pass[h * half : (h + 1) * half, 0:kr] = crosses.astype(NARROW)
         wide = half
         pair = jnp.concatenate([under[:, i * wide : (i + 1) * wide] for i in range(under.shape[1] // wide)], axis=0)
         for i in range(own_j // 2):
@@ -505,8 +558,9 @@
 
         h_pass(g).wait_recv()
     for e in range(n_in - 1):
-        y_inner(e).wait_recv()
-        y_pass(e).start()
+        for k in range(slots):
+            y_inner(e, k).wait_recv()
+            y_pass(e, k).start()
     for j in range(own_j):
         rows = slice(j * rank, (j + 1) * rank)
         both = jnp.concatenate(split(inv[j]), axis=0)
@@ -518,12 +572,13 @@
     for j in range(own_j):
         rows = slice(j * rank, (j + 1) * rank)
         crossed = jnp.concatenate(
-            [cross_sum[rows, 0:kr]] + [cross_got[e, rows, 0:kr] for e in range(n_in - 1)], axis=1
+            [cross_sum[rows, 0:kr]] + [cross_got[e, rows, 0:kr].astype(WIDE) for e in range(n_in - 1)], axis=1
         )
         projected = jnp.dot(inv[j], crossed, precision=HIGHEST, preferred_element_type=WIDE)
         left.append(jnp.concatenate(split(projected), axis=0))
     for e in range(n_in - 1):
-        y_pass(e).wait_recv()
+        for k in range(slots):
+            y_pass(e, k).wait_recv()
     lane_own = pl.ds(pl.multiple_of(inner * share, share), share)
     for j in range(own_j):
         rows = slice(j * rank, (j + 1) * rank)
@@ -532,15 +587,23 @@
         out = jnp.dot(left[j], jnp.concatenate(right, axis=0), preferred_element_type=WIDE)
         coupling_ref[j] = out[:rank] + out[rank:]
 
-    for p in range(planes):
-        y_twin(p).wait_send()
-    for f in range(planes - 1):
-        y_far(f).wait_send()
+    for k in range(slots):
+        for p in range(planes):
+            y_twin(p, k).wait_send()
+        for f in range(planes - 1):
+            y_far(f, k).wait_send()
+            for way in range(2):
+
+                @pl.when(beside[way])
+                def _(f=f, k=k, way=way):
+                    x_side(k, f, way).wait_send()
+
     for d in range(n_row - 1):
         z_piece(d).wait_send()
     for e in range(n_in - 1):
-        y_inner(e).wait_send()
-        y_pass(e).wait_send()
+        for k in range(slots):
+            y_inner(e, k).wait_send()
+            y_pass(e, k).wait_send()
         c_inner(e).wait_send()
     for g in range(group):
         h_pass(g).wait_send()
@@ -557,15 +620,19 @@
 
         for f in range(planes - 1):
             z_far(s, f).wait_send()
-            for k in range(slots):
-                x_far(s, k, f).wait_send()
+
+            @pl.when(jnp.logical_not(jnp.logical_and(middle, jnp.logical_or(s == col - 1, s == col + 1))))
+            def _(f=f):
+                for k in range(slots):
+                    x_far(s, k, f).wait_send()
+
         for p in range(planes):
             z_twin(s, p).wait_send()
             for k in range(slots):
                 x_twin(s, k, p).wait_send()
         for e in range(n_in - 1):
-            for h in range(2):
-                s_peer(s, h, e).wait_send()
+            for j in range(own_j):
+                s_peer(s, j, e).wait_send()
 
         @pl.when(s != col)
         def _():
@@ -600,59 +667,64 @@
     dma = pltpu.SemaphoreType.DMA
     dims = (n_row, n_col, n_in, slots, own_j, rank, width, cols)
     out = jax.ShapeDtypeStruct((own_j, rank, share), WIDE)
+    buffers = [
+        (u.shape, NARROW),
+        ((own_j, rank, width), NARROW),
+        ((slots, n_col * js, total), NARROW),
+        ((slots, rank, total), NARROW),
+        ((slots, js, total), NARROW),
+        ((n_in - 1, slots, js, share), NARROW),
+        ((slots, total, cols), NARROW),
+        ((n_col, own_j, kr, cols), NARROW),
+        ((n_col, js, lanes(kr)), NARROW),
+        ((js, lanes(kr)), WIDE),
+        ((n_row - 1, js // n_row, lanes(kr)), WIDE),
+        ((js // n_row, lanes(kr)), NARROW),
+        ((n_col, js, cols), WIDE),
+        ((n_col, js, cols), NARROW),
+        ((n_in - 1, n_col, js, cols), NARROW),
+        ((n_col, 2, packed, kr + rank), NARROW),
+        ((n_col, 2, packed, kr + rank), NARROW),
+        ((n_col, js, cols), NARROW),
+        ((group, half, cols), NARROW),
+        ((js, share), NARROW),
+        ((js, lanes(kr)), WIDE),
+        ((js, lanes(kr)), NARROW),
+        ((n_in - 1, js, lanes(kr)), NARROW),
+        ((own_j, rank, rank), WIDE),
+    ]
+    held = sum(math.prod(shape) * jnp.dtype(kind).itemsize for shape, kind in buffers)
     return pl.pallas_call(
         functools.partial(product_kernel, dims),
         out_shape=(out, out),
-        in_specs=[
-            pl.BlockSpec(memory_space=pltpu.SMEM), vmem, vmem, pl.BlockSpec(memory_space=pltpu.HBM), vmem, vmem, vmem
-        ],
+        in_specs=[pl.BlockSpec(memory_space=pltpu.SMEM)] + [pl.BlockSpec(memory_space=pltpu.HBM)] * 6,
         out_specs=[vmem] * 2,
-        scratch_shapes=[
-            pltpu.VMEM((slots, n_col * js, total), NARROW),
-            pltpu.VMEM((slots, rank, total), NARROW),
-            pltpu.VMEM((slots, js, total), NARROW),
-            pltpu.VMEM((n_in - 1, slots, js, share), NARROW),
-            pltpu.VMEM((slots, total, cols), NARROW),
-            pltpu.VMEM((n_col, own_j, kr, cols), NARROW),
-            pltpu.VMEM((n_col, js, lanes(kr)), NARROW),
-            pltpu.VMEM((js, lanes(kr)), WIDE),
-            pltpu.VMEM((n_row - 1, js // n_row, lanes(kr)), WIDE),
-            pltpu.VMEM((js // n_row, lanes(kr)), NARROW),
-            pltpu.VMEM((n_col, js, cols), WIDE),
-            pltpu.VMEM((n_col, js, cols), NARROW),
-            pltpu.VMEM((n_in - 1, n_col, js, cols), NARROW),
-            pltpu.VMEM((n_col, 2, packed, kr + rank), NARROW),
-            pltpu.VMEM((n_col, 2, packed, kr + rank), NARROW),
-            pltpu.VMEM((n_col, js, cols), NARROW),
-            pltpu.VMEM((group, half, cols), NARROW),
-            pltpu.VMEM((js, share), NARROW),
-            pltpu.VMEM((js, lanes(kr)), WIDE),
-            pltpu.VMEM((n_in - 1, js, lanes(kr)), WIDE),
-            pltpu.VMEM((own_j, rank, rank), WIDE),
+        scratch_shapes=[pltpu.VMEM(*buffer) for buffer in buffers] + [
             dma((2, n_col, slots)), dma((n_col, slots)),
             dma((planes - 1, n_col, slots)), dma((planes - 1, n_col, slots)),
             dma((planes, n_col, slots)), dma((planes, n_col, slots)),
+            dma((planes - 1, 2, slots)), dma((planes - 1, 2, slots)),
             dma((2, n_col)), dma((n_col,)),
             dma((2, n_col)), dma((n_col,)),
             dma((planes - 1, n_col)), dma((planes - 1, n_col)),
             dma((planes, n_col)), dma((planes, n_col)),
             dma((n_row - 1,)), dma((n_row - 1,)),
-            dma((n_in - 1, n_col, 2)), dma((n_in - 1, n_col, 2)),
+            dma((n_in - 1, n_col, own_j)), dma((n_in - 1, n_col, own_j)),
             dma((n_col, 2)), dma((n_col, 2)),
             dma((n_col,)), dma((group,)),
             dma((n_col,)), dma((group,)),
             dma((group,)), dma((group,)),
-            dma((planes - 1,)), dma((planes - 1,)),
-            dma((planes,)), dma((planes,)),
+            dma((planes - 1, slots)), dma((planes - 1, slots)),
+            dma((planes, slots)), dma((planes, slots)),
+            dma((n_in - 1, slots)), dma((n_in - 1, slots)),
+            dma((n_in - 1, slots)), dma((n_in - 1, slots)),
             dma((n_in - 1,)), dma((n_in - 1,)),
-            dma((n_in - 1,)), dma((n_in - 1,)),
-            dma((n_in - 1,)), dma((n_in - 1,)),
-            dma((slots,)),
+            dma((slots,)), dma((slots,)), dma((slots,)), dma((3,)),
         ],
         compiler_params=pltpu.CompilerParams(
-            collective_id=0, has_side_effects=True, vmem_limit_bytes=60 * 1024 * 1024
+            collective_id=0, has_side_effects=True, vmem_limit_bytes=held + 6 * 1024 * 1024
         ),
-    )(flags, u, v, d, x, y, omega)
+    )(flags, *[pltpu.with_memory_space_constraint(part, pltpu.HBM) for part in (u, v, d, x, y, omega)])
 
 
 def inverse_factor(gram, out_ref):

time: 146 us -> 139 us (0.952); the launches traced: 145 us -> 137 us
  Pallas kernels: 140 us -> 133 us
    pallas_call x1, Pallas kernels: 140 us -> 133 us  [product(): pl.pallas_call(functools.partial(product_kernel, dims), out_shape=(out, o...]
where the time goes in v3:
time: 139 us; the launch traced here: 137 us
  Pallas kernels  133 us (96%)
  local copies, waits for them, and re-layouts  1.62 us (1%)
    pallas_call x1, Pallas kernels, product(): pl.pallas_call(functools.partial(product_kernel, dims), out_shape=(out, o...  133 us

profile of v3, /device:TPU:0, one launch (start us, length us, event | category | flops | bytes accessed | tf_op | source)
XLA Modules:
  0.0 136.8 jit_solution(3354958573897394971)
XLA Ops:
  0.6 0.0 copy-start
  0.6 0.6 copy-done
  1.3 133.5 %shard_map.86 = (f32[4,64,1024]{2,1,0:T(8,128)S(1)}, f32[4,64,1024]{2,1,0:T(8,128)S(1)}) custom-call(s32[1,3]{1,0:T(1,128)S(1)} %copy-done, bf16[3,64,512]{2,1,0:T(8,128)(2,1)} %bitcast.12, bf16[3,64,512]{2,1,0:T(8,128)(2,1)} %bitcast.13, bf16[3,2048,512]{2,1,0:T(8,128)(2,1)} %bitcast.9, bf16[3,256,512]{2,1,0:T(8,128)(2,1)} %bitcast.10, ...), custom_call_target="tpu_custom_call" | custom-call | tf_op jit(solution)/shard_map/pallas_call | solution.py:697
  134.8 1.1 multiply_bitcast_fusion
  135.9 1.0 copy.10
Async XLA Ops:
  0.6 0.7 copy-start

commit v4 on v3

--- a/solution.py
+++ b/solution.py
@@ -47,7 +47,8 @@
     x_z_send, x_z_recv, x_f_send, x_f_recv, x_t_send, x_t_recv, x_s_send, x_s_recv,
     v_send, v_recv, z_z_send, z_z_recv, z_f_send, z_f_recv, z_t_send, z_t_recv, zp_send, zp_recv,
     s_send, s_recv, m_send, m_recv, h_send, h_recv, r_send, r_recv, f_send, f_recv,
-    y_f_send, y_f_recv, y_t_send, y_t_recv, y_y_send, y_y_recv, y_p_send, y_p_recv, c_send, c_recv, own, x_own, y_own, v_own,
+    y_f_send, y_f_recv, y_t_send, y_t_recv, y_y_send, y_y_recv, y_p_send, y_p_recv, c_send, c_recv,
+    w_send, w_recv, own, x_own, y_own, v_own,
 ):
     n_row, n_col, n_in, slots, own_j, rank, width, cols = dims
     js = own_j * rank
@@ -149,6 +150,15 @@
     def share_plane(peer):
         return lax.div(peer * share, 2 * width)
 
+    def y_cross(f, e):
+        place = yb.at[e, slots - 1, mine]
+        return remote(place, place, w_send.at[f, e], w_recv.at[f, e], fars[f])
+
+    own_share = share_plane(inner) == plane
+
+    def crosses_back(f, k):
+        return True if k < slots - 1 else share_plane(inner) == back_planes[f]
+
     def s_peer(s, j, e):
         rows = pl.ds(j * rank, rank)
         return remote(
@@ -224,8 +234,7 @@
         def _(way=way):
             v_line(col, way).start()
 
-    for k in range(min(2, slots)):
-        own_line(k)
+    own_line(0)
     for f in range(planes - 1):
         x_far(col, 0, f).start()
     for k in range(slots):
@@ -463,33 +472,54 @@
     def start_y():
         for f in range(planes - 1):
             for k in range(slots):
-                y_far(f, k).start()
+
+                @pl.when(own_share if k == slots - 1 else True)
+                def _(f=f, k=k):
+                    y_far(f, k).start()
+
+    def cross_y():
+        @pl.when(own_share)
+        def _():
+            for e in range(n_in - 1):
+                y_inner(e, slots - 1).wait_recv()
+                for f in range(planes - 1):
+                    y_cross(f, e).start()
 
     def pass_y():
         for k in range(slots):
             for f in range(planes - 1):
-                y_far(f, k).wait_recv()
-                y_twin(back_planes[f], k).start()
+
+                @pl.when(crosses_back(f, k))
+                def _(f=f, k=k):
+                    y_far(f, k).wait_recv()
+                    y_twin(back_planes[f], k).start()
+
             for f in range(planes - 1):
-                y_twin(back_planes[f], k).wait_recv()
-            for e in range(n_in - 1):
-
-                @pl.when(share_plane(in_peers[e]) != plane)
-                def _(e=e, k=k):
-                    y_inner(e, k).start()
+
+                @pl.when(crosses_back(f, k))
+                def _(f=f, k=k):
+                    y_twin(back_planes[f], k).wait_recv()
+
+            if k < slots - 1:
+                for e in range(n_in - 1):
+
+                    @pl.when(share_plane(in_peers[e]) != plane)
+                    def _(e=e, k=k):
+                        y_inner(e, k).start()
 
     def step(q, carry):
+        @pl.when(q < n_col - 1)
+        def _():
+            along(q + 1, pass_v)
+
+        @pl.when(q + 1 < slots)
+        def _():
+            own_line(q + 1)
+
         @pl.when(q < count)
         def _():
             pump(lax.div(q, slots), lax.rem(q, slots))
 
-        @pl.when(q < n_col - 1)
-        def _():
-            along(q + 1, pass_v)
-
-        @pl.when(q + 2 < slots)
-        def _():
-            own_line(q + 2)
 
         @pl.when(q == 0)
         def _():
@@ -498,6 +528,10 @@
         @pl.when(q == jnp.where(middle, 0, (n_col - 1) * slots))
         def _():
             start_y()
+
+        @pl.when(q == jnp.where(middle, 2 * slots, (n_col - 1) * slots))
+        def _():
+            cross_y()
 
         @pl.when(jnp.logical_and(middle, q == 2 * slots))
         def _():
@@ -558,9 +592,16 @@
 
         h_pass(g).wait_recv()
     for e in range(n_in - 1):
-        for k in range(slots):
+        for k in range(slots - 1):
             y_inner(e, k).wait_recv()
             y_pass(e, k).start()
+        for f in range(planes - 1):
+
+            @pl.when(share_plane(inner) == back_planes[f])
+            def _(e=e, f=f):
+                y_cross(f, e).wait_recv()
+
+        y_pass(e, slots - 1).start()
     for j in range(own_j):
         rows = slice(j * rank, (j + 1) * rank)
         both = jnp.concatenate(split(inv[j]), axis=0)
@@ -588,10 +629,17 @@
         coupling_ref[j] = out[:rank] + out[rank:]
 
     for k in range(slots):
-        for p in range(planes):
-            y_twin(p, k).wait_send()
+        y_twin(plane, k).wait_send()
         for f in range(planes - 1):
-            y_far(f, k).wait_send()
+
+            @pl.when(crosses_back(f, k))
+            def _(f=f, k=k):
+                y_twin(back_planes[f], k).wait_send()
+
+            @pl.when(own_share if k == slots - 1 else True)
+            def _(f=f, k=k):
+                y_far(f, k).wait_send()
+
             for way in range(2):
 
                 @pl.when(beside[way])
@@ -602,8 +650,18 @@
         z_piece(d).wait_send()
     for e in range(n_in - 1):
         for k in range(slots):
-            y_inner(e, k).wait_send()
             y_pass(e, k).wait_send()
+
+            @pl.when(share_plane(in_peers[e]) == plane if k == slots - 1 else True)
+            def _(e=e, k=k):
+                y_inner(e, k).wait_send()
+
+        for f in range(planes - 1):
+
+            @pl.when(own_share)
+            def _(e=e, f=f):
+                y_cross(f, e).wait_send()
+
         c_inner(e).wait_send()
     for g in range(group):
         h_pass(g).wait_send()
@@ -719,6 +777,7 @@
             dma((n_in - 1, slots)), dma((n_in - 1, slots)),
             dma((n_in - 1, slots)), dma((n_in - 1, slots)),
             dma((n_in - 1,)), dma((n_in - 1,)),
+            dma((planes - 1, n_in - 1)), dma((planes - 1, n_in - 1)),
             dma((slots,)), dma((slots,)), dma((slots,)), dma((3,)),
         ],
         compiler_params=pltpu.CompilerParams(

time: 139 us -> 133 us (0.957); the launches traced: 137 us -> 133 us
  Pallas kernels: 133 us -> 129 us
    pallas_call x1, Pallas kernels: 133 us -> 129 us  [product(): pl.pallas_call(functools.partial(product_kernel, dims), out_shape=(out, o...]
where the time goes in v4:
time: 133 us
  Pallas kernels  129 us (97%)
  local copies, waits for them, and re-layouts  1.62 us (1%)
    pallas_call x1, Pallas kernels, product(): pl.pallas_call(functools.partial(product_kernel, dims), out_shape=(out, o...  129 us

profile of v4, /device:TPU:0, one launch (start us, length us, event | category | flops | bytes accessed | tf_op | source)
XLA Modules:
  0.0 132.8 jit_solution(13796674101059797620)
XLA Ops:
  0.6 0.0 copy-start
  0.6 0.6 copy-done
  1.3 129.5 %shard_map.86 = (f32[4,64,1024]{2,1,0:T(8,128)S(1)}, f32[4,64,1024]{2,1,0:T(8,128)S(1)}) custom-call(s32[1,3]{1,0:T(1,128)S(1)} %copy-done, bf16[3,64,512]{2,1,0:T(8,128)(2,1)} %bitcast.12, bf16[3,64,512]{2,1,0:T(8,128)(2,1)} %bitcast.13, bf16[3,2048,512]{2,1,0:T(8,128)(2,1)} %bitcast.9, bf16[3,256,512]{2,1,0:T(8,128)(2,1)} %bitcast.10, ...), custom_call_target="tpu_custom_call" | custom-call | tf_op jit(solution)/shard_map/pallas_call | solution.py:755
  130.8 1.1 multiply_bitcast_fusion
  131.8 1.0 copy.10
Async XLA Ops:
  0.6 0.7 copy-start
